TPU v7x, 512 devices: a whole 4x8x8 slice. The times are simulated.
512 devices in a mesh: row: 16 (over y_lo, x, core), col: 32 (over y_hi, z).
Axes of the slice: x: 4, y: 8 (y_hi: 4, y_lo: 2; y = y_hi * 2 + y_lo), z: 8, core: 2. Of those that a mesh axis runs over, the one named last changes fastest.
Arguments:
- object_field: float32 [2, 4096, 8192], P(None, 'row', 'col'), may hold values from -6 to 6
- probe: float32 [2, 128, 128], replicated, may hold values from -6 to 6
- amplitude: bfloat16 [16, 32, 16, 128, 128], P('row', 'col'), may hold values from 0 to 2
- corners: int32 [2, 16, 32, 16], P(None, 'row', 'col'), may hold values from 0 to 255, as said below
- live_count: int32 [16, 32], P('row', 'col'), may hold values from 4 to 16, as said below
Outputs:
- refined_object: float32 [2, 4096, 8192], P(None, 'row', 'col')
- new_probe: float32 [2, 128, 128], replicated
Inputs may be any that keep to these rules, and one draw needn't show every extreme that they name: In the last tile row of the mesh corners[0] is at most 128, and in the last tile column corners[1] is at most 128, so every window lies inside the object. Outside the last tile row, corners[0] of slot 0 is at least 192; outside the last tile column, corners[1] of slot 0 is at least 192. Unused slots carry valid corners. Slots from live_count on are unused. Some tile uses all 16 slots in every draw.
All inputs are finite; a program needn't handle non-finite values.
Results may differ from a plain program's by a relative error of at most 0.0039.
The roundings to bfloat16 on the way count: a program that leaves them out, or rounds other values in their place, can miss the bound.
Values may be sent and summed in bfloat16 or wider, within the bound.
No kernel may reach another device: no remote copies, remote signals or barrier semaphores. Data moves between devices by JAX's collectives and lax.ppermute only.
A program may use at most 64 MiB of HBM per device.

v0:
```python
import math

import jax
import jax.numpy as jnp
from jax import lax
from jax.experimental import pallas as pl
from jax.experimental.pallas import tpu as pltpu
from jax.sharding import PartitionSpec as P


GROUP = 8
F32 = jnp.float32
BF16 = jnp.bfloat16
HALO = BF16
TERMS = BF16
GRAD = BF16


def shift(value, axis, steps):
    count = lax.axis_size(axis)
    first, last = (max(0, -steps), min(count, count - steps))
    return lax.ppermute(value, axis, [(source, source + steps) for source in range(first, last)])


def dft_tables(window):
    indices = jnp.arange(window, dtype=jnp.int32)
    phase_index = indices[:, None] * indices[None, :] % window
    angles = phase_index.astype(F32) * (2.0 * math.pi / window)
    norming = 1.0 / math.sqrt(window)
    cosines = jnp.cos(angles) * norming
    sines = jnp.sin(angles) * norming
    turned = jnp.block([[cosines, sines], [-sines, cosines]])
    straight = jnp.block([[cosines, -sines], [sines, cosines]])
    return jnp.stack([straight, turned]).astype(BF16)


def dot(left, right):
    return lax.dot_general(left, right, (((1,), (0,)), ((), ())), preferred_element_type=F32)


def accumulate(ref, lead, block, row, turn, lanes, value):
    turned = pltpu.roll(value, turn, 1)
    window = value.shape[0]
    inner = lanes >= turn
    rows = pl.ds(row, window)
    ref[lead, block, rows, :] += jnp.where(inner, turned, 0.0)
    ref[lead, block + 1, rows, :] += jnp.where(inner, 0.0, turned)


def sweep_slots(
    live_ref, corners_ref, ext_ref, probe_ref, amp_ref, tab_ref,
    dep_ref, grad_ref, power_ref, patch_ref, wave_ref, with_light,
):
    window = probe_ref.shape[1]
    live = live_ref[0, 0]
    lanes = lax.broadcasted_iota(jnp.int32, (window, window), 1)
    straight = tab_ref[0]
    turned = tab_ref[1]

    def step(index, carry):
        base = index * GROUP
        spots = []
        waves = []
        for member in range(GROUP):
            slot = base + member
            row = corners_ref[0, slot]
            col = corners_ref[1, slot]
            block = col // window
            turn = col - block * window
            spots.append((slot, row, block, turn))
            back = jnp.where(turn == 0, 0, window - turn)
            inside = lanes < window - turn
            rows = pl.ds(row, window)
            pieces = []
            for part in range(2):
                near = pltpu.roll(ext_ref[part, block, rows, :], back, 1)
                far = pltpu.roll(ext_ref[part, block + 1, rows, :], back, 1)
                pieces.append(jnp.where(inside, near, far))
            if not with_light:
                patch_ref[member, 0] = pieces[0]
                patch_ref[member, 1] = pieces[1]
            pr, pi = probe_ref[0], probe_ref[1]
            real = (pr * pieces[0] - pi * pieces[1]).astype(BF16)
            imag = (pr * pieces[1] + pi * pieces[0]).astype(BF16)
            wave = jnp.concatenate([real, imag], 1)
            wave_ref[member] = wave
            waves.append(wave)
        pairs = [(m, m + 1) for m in range(0, GROUP, 2)]

        def beside(parts):
            return jnp.concatenate(
                [jnp.concatenate([h[:, :window], h[:, window:]], 0) for h in parts], 1
            )

        half = [[dot(waves[m], straight).astype(BF16) for m in ms] for ms in pairs]
        spectra = [dot(turned, beside(h)) for h in half]
        back = []
        for ms, spectrum in zip(pairs, spectra):
            projected = []
            for place, m in enumerate(ms):
                lo = place * window
                sr = spectrum[:window, lo : lo + window]
                si = spectrum[window:, lo : lo + window]
                amp = amp_ref[base + m].astype(F32)
                scale = amp * lax.rsqrt(jnp.maximum(sr * sr + si * si, 0.25))
                projected.append(
                    jnp.concatenate([(sr * scale).astype(BF16), (si * scale).astype(BF16)], 1)
                )
            back.append([dot(p, turned).astype(BF16) for p in projected])
        for ms, h in zip(pairs, back):
            returned = dot(straight, beside(h))
            for place, m in enumerate(ms):
                slot, row, block, turn = spots[m]
                weight = jnp.where(slot < live, 1.0, 0.0).astype(F32)
                lo = place * window
                wave = wave_ref[m].astype(F32)
                cr = (returned[:window, lo : lo + window] - wave[:, :window]) * weight
                ci = (returned[window:, lo : lo + window] - wave[:, window:]) * weight
                pr, pi = probe_ref[0], probe_ref[1]
                accumulate(dep_ref, 0, block, row, turn, lanes, pr * cr + pi * ci)
                accumulate(dep_ref, 1, block, row, turn, lanes, pr * ci - pi * cr)
                if with_light:
                    accumulate(dep_ref, 2, block, row, turn, lanes, power_ref[...] * weight)
                else:
                    xr, xi = patch_ref[m, 0], patch_ref[m, 1]
                    grad_ref[0] += xr * cr + xi * ci
                    grad_ref[1] += xr * ci - xi * cr
        return carry

    lax.fori_loop(0, (live + GROUP - 1) // GROUP, step, 0)


def first_kernel(
    live_ref, corners_ref, obj_ref, right_ref, low_ref, corner_ref, probe_ref, amp_ref, tab_ref,
    ext_ref, dep_ref, to_right_ref, to_left_ref, power_ref, patch_ref, wave_ref,
):
    window = probe_ref.shape[1]
    tile = obj_ref.shape[1]
    for part in range(2):
        for block in range(2):
            cols = slice(block * window, (block + 1) * window)
            ext_ref[part, block, 0:tile, :] = obj_ref[part, :, cols]
            ext_ref[part, block, tile:, :] = low_ref[part, :, cols].astype(F32)
        ext_ref[part, 2, 0:tile, :] = right_ref[part].astype(F32)
        ext_ref[part, 2, tile:, :] = corner_ref[part].astype(F32)
    dep_ref[...] = jnp.zeros(dep_ref.shape, F32)
    power_ref[...] = probe_ref[0] * probe_ref[0] + probe_ref[1] * probe_ref[1]
    sweep_slots(
        live_ref, corners_ref, ext_ref, probe_ref, amp_ref, tab_ref,
        dep_ref, None, power_ref, patch_ref, wave_ref, True,
    )
    for part in range(3):
        to_right_ref[part] = dep_ref[part, 2].astype(TERMS)
        to_left_ref[part] = dep_ref[part, 0].astype(TERMS)


def middle_kernel(dep_ref, from_left_ref, from_right_ref, down_ref, up_ref):
    window = from_left_ref.shape[2]
    tile = from_left_ref.shape[1] - window
    for part in range(3):
        for ref, rows in ((down_ref, slice(tile, tile + window)), (up_ref, slice(0, window))):
            ref[part, 0] = (dep_ref[part, 0, rows, :] + from_left_ref[part, rows, :].astype(F32)).astype(TERMS)
            ref[part, 1] = dep_ref[part, 1, rows, :].astype(TERMS)
            ref[part, 2] = (dep_ref[part, 2, rows, :] + from_right_ref[part, rows, :].astype(F32)).astype(TERMS)


def second_kernel(
    live_ref, corners_ref, ext_ref, dep_in_ref, left_ref, right_ref, above_ref, below_ref,
    probe_ref, amp_ref, tab_ref,
    upd_ref, den_ref, dep_ref, to_right_ref, grad_ref, sum_ref, patch_ref, wave_ref,
):
    window = probe_ref.shape[1]
    total = ext_ref.shape[2]
    tile = total - window
    for block in range(3):
        for first in range(0, total, window):
            rows = slice(first, first + window)
            sums = []
            for part in (2, 0, 1):
                value = dep_in_ref[part, block, rows, :]
                if block == 0:
                    value = value + left_ref[part, rows, :].astype(F32)
                if block == 2:
                    value = value + right_ref[part, rows, :].astype(F32)
                if first == 0:
                    value = value + above_ref[part, block].astype(F32)
                if first == tile:
                    value = value + below_ref[part, block].astype(F32)
                sums.append(value)
            inverse = 1.0 / (sums[0] + 4.0)
            for part in range(2):
                upd_ref[part, block, rows, :] = ext_ref[part, block, rows, :] + sums[part + 1] * inverse
            if first < tile and block < 2:
                den_ref[block, rows, :] = inverse
    dep_ref[...] = jnp.zeros(dep_ref.shape, F32)
    grad_ref[...] = jnp.zeros(grad_ref.shape, F32)
    sweep_slots(
        live_ref, corners_ref, upd_ref, probe_ref, amp_ref, tab_ref,
        dep_ref, grad_ref, None, patch_ref, wave_ref, False,
    )
    for part in range(2):
        to_right_ref[part] = dep_ref[part, 2].astype(TERMS)


def finish_kernel(upd_ref, den_ref, dep_ref, left_ref, above_ref, out_ref):
    window = left_ref.shape[2]
    tile = out_ref.shape[1]
    for part in range(2):
        for block in range(2):
            cols = slice(block * window, (block + 1) * window)
            for first in range(0, tile, window):
                rows = slice(first, first + window)
                value = dep_ref[part, block, rows, :]
                if block == 0:
                    value = value + left_ref[part, rows, :].astype(F32)
                if first == 0:
                    value = value + above_ref[part, block].astype(F32)
                out_ref[part, rows, cols] = (
                    upd_ref[part, block, rows, :] + value * den_ref[block, rows, :]
                )


def probe_kernel(probe_ref, sum_ref, out_ref):
    summed = sum_ref[...]
    power = jnp.sum(summed * summed, axis=(0, 1, 2), keepdims=True)
    scale = 1.0 / jnp.sqrt(power / (out_ref.shape[1] * out_ref.shape[2]) + 1e-06)
    out_ref[...] = probe_ref[...] + summed * scale


VM = pl.BlockSpec(memory_space=pltpu.VMEM)
SM = pl.BlockSpec(memory_space=pltpu.SMEM)


def call(kernel, shapes, in_specs, scratch=(), flops=10**6):
    return pl.pallas_call(
        kernel,
        out_shape=[jax.ShapeDtypeStruct(shape, kind) for shape, kind in shapes],
        in_specs=in_specs,
        out_specs=[VM] * len(shapes),
        scratch_shapes=scratch,
        compiler_params=pltpu.CompilerParams(vmem_limit_bytes=40 * 2**20),
        cost_estimate=pl.CostEstimate(flops=flops, transcendentals=0, bytes_accessed=10**6),
    )


def exchange(parts, axis):
    return lax.all_to_all(parts, axis, 0, 0, tiled=True)


def sweeps(object_field, probe, amplitude, corners, live_count):
    slots = amplitude.shape[2]
    window = probe.shape[1]
    tile = object_field.shape[1]
    wide = tile + window
    across = lax.axis_size("col")
    amp = amplitude.reshape(slots, window, window)
    spots = corners.reshape(2, slots)
    live = live_count.reshape(1, 1)
    tables = dft_tables(window)

    right = shift(object_field[:, :, :window].astype(HALO), "col", -1)
    low = shift(object_field[:, :window, :].astype(HALO), "row", -1)
    diagonal = shift(
        object_field[:, :window, :window].astype(HALO), ("row", "col"), -(across + 1)
    )
    scratch = [
        pltpu.VMEM((window, window), F32),
        pltpu.VMEM((GROUP, 2, window, window), F32),
        pltpu.VMEM((GROUP, window, 2 * window), BF16),
    ]
    ext, dep, to_right, to_left = call(
        first_kernel,
        [
            ((2, 3, wide, window), F32),
            ((3, 3, wide, window), F32),
            ((3, wide, window), TERMS),
            ((3, wide, window), TERMS),
        ],
        [SM, SM] + [VM] * 7,
        scratch,
        10**9,
    )(live, spots, object_field, right, low, diagonal, probe, amp, tables)

    from_left = shift(to_right, "col", 1)
    from_right = shift(to_left, "col", -1)
    down, up = call(
        middle_kernel, [((3, 3, window, window), TERMS), ((3, 3, window, window), TERMS)], [VM] * 3
    )(dep, from_left, from_right)
    from_above = shift(down, "row", 1)
    from_below = shift(up, "row", -1)

    updated, inverse, dep, to_right, gradient = call(
        second_kernel,
        [
            ((2, 3, wide, window), F32),
            ((2, tile, window), F32),
            ((2, 3, wide, window), F32),
            ((2, wide, window), TERMS),
            ((2, window, window), F32),
        ],
        [SM, SM] + [VM] * 9,
        scratch,
        10**9,
    )(live, spots, ext, dep, from_left, from_right, from_above, from_below, probe, amp, tables)

    rows, cols = lax.axis_size("row"), lax.axis_size("col")
    parts = exchange(gradient.astype(GRAD).reshape(rows, -1, window), "row")
    part = jnp.sum(parts.astype(F32), 0).astype(GRAD)
    to_right, dep, ignored = lax.optimization_barrier((to_right, dep, part))
    parts = exchange(jnp.broadcast_to(part[None], (cols,) + part.shape), "col")
    from_left = shift(to_right, "col", 1)
    spill = dep[:, :2, tile:, :]
    spill = jnp.concatenate(
        [(spill[:, :1] + from_left[:, None, tile:].astype(F32)), spill[:, 1:]], 1
    ).astype(TERMS)
    part = jnp.sum(parts.astype(F32), 0)
    spill, ignored = lax.optimization_barrier((spill, part))
    parts = exchange(jnp.broadcast_to(part[None], (rows,) + part.shape), "row")
    from_above = shift(spill, "row", 1)
    refined = call(
        finish_kernel, [((2, tile, tile), F32)], [VM] * 5
    )(updated, inverse, dep, from_left, from_above)[0]
    new_probe = call(probe_kernel, [(probe.shape, F32)], [VM] * 2)(
        probe, parts.reshape(gradient.shape)
    )[0]
    return (refined, new_probe)


def solution(mesh):
    in_specs = (
        P(None, "row", "col"),
        P(),
        P("row", "col", None, None, None),
        P(None, "row", "col", None),
        P("row", "col"),
    )
    out_specs = (P(None, "row", "col"), P())
    return jax.shard_map(sweeps, mesh=mesh, in_specs=in_specs, out_specs=out_specs, check_vma=False)
```

profile of v0, /device:TPU:8, one launch (start us, length us, event | category | flops | bytes accessed | tf_op | source)
XLA Modules:
  0.0 116.7 jit_solution(9219042252240275469)
XLA Ops:
  0.7 1.2 convert.46
  1.8 16.7 %collective-permute-start.2 = (bf16[2,128,128]{2,1,0:T(8,128)(2,1)S(1)}, bf16[2,128,128]{2,1,0:T(8,128)(2,1)S(1)}, u32[]{:S(2)}, u32[]{:S(2)}) collective-permute-start(bf16[2,128,128]{2,1,0:T(8,128)(2,1)S(1)} %slice.33), channel_id=1, source_target_pairs={{33,0},{34,1},{35,2},{36,3},{37,4},{38,5},{39,6},{40,7},{41,8},{42... | collective-permute-start | bytes 196616 | tf_op jit(solution)/shard_map/ppermute | solution.py:22
  18.6 1.3 %collective-permute-start = (bf16[2,256,128]{2,1,0:T(8,128)(2,1)S(1)}, bf16[2,256,128]{2,1,0:T(8,128)(2,1)S(1)}, u32[]{:S(2)}, u32[]{:S(2)}) collective-permute-start(bf16[2,256,128]{2,1,0:T(8,128)(2,1)S(1)} %slice.31), channel_id=1, source_target_pairs={{1,0},{2,1},{3,2},{4,3},{5,4},{6,5},{7,6},{8,7},{9,8},{10,9},{11,1... | collective-permute-start | bytes 393224 | tf_op jit(solution)/shard_map/ppermute | solution.py:22
  19.9 1.9 %collective-permute-start.1 = (bf16[2,128,256]{2,1,0:T(8,128)(2,1)S(1)}, bf16[2,128,256]{2,1,0:T(8,128)(2,1)S(1)}, u32[]{:S(2)}, u32[]{:S(2)}) collective-permute-start(bf16[2,128,256]{2,1,0:T(8,128)(2,1)S(1)} %slice.32), channel_id=1, source_target_pairs={{32,0},{64,32},{96,64},{128,96},{160,128},{192,160},{224,192},{256... | collective-permute-start | bytes 393224 | tf_op jit(solution)/shard_map/ppermute | solution.py:22
  23.1 2.3 %collective-permute-done.right_ref = bf16[2,256,128]{2,1,0:T(8,128)(2,1)S(1)} collective-permute-done((bf16[2,256,128]{2,1,0:T(8,128)(2,1)S(1)}, bf16[2,256,128]{2,1,0:T(8,128)(2,1)S(1)}, u32[]{:S(2)}, u32[]{:S(2)}) %collective-permute-start) | collective-permute-done | bytes 131104 | tf_op jit(solution)/shard_map/ppermute | solution.py:22
  25.5 2.7 %shard_map.68 = (f32[2,3,384,128]{3,2,1,0:T(8,128)S(1)}, f32[3,3,384,128]{3,2,1,0:T(8,128)S(1)}, bf16[3,384,128]{2,1,0:T(8,128)(2,1)S(1)}, bf16[3,384,128]{2,1,0:T(8,128)(2,1)S(1)}) custom-call(s32[1,1]{1,0:T(1,128)S(6)} %copy.7.live_ref, s32[2,16]{1,0:T(2,128)S(1)} %bitcast.16, f32[2,256,256]{2,1,0:T(8,128)S(1)} %copy-done.2, ...), custom_call_target="tpu_custom_call" | custom-call | flops 1000000000 | bytes 1000000 | tf_op jit(solution)/shard_map/pallas_call | solution.py:271
  28.2 3.4 %collective-permute-start.3 = (bf16[3,384,128]{2,1,0:T(8,128)(2,1)S(1)}, bf16[3,384,128]{2,1,0:T(8,128)(2,1)S(1)}, u32[]{:S(2)}, u32[]{:S(2)}) collective-permute-start(bf16[3,384,128]{2,1,0:T(8,128)(2,1)S(1)} %get-tuple-element.18), channel_id=1, source_target_pairs={{0,1},{1,2},{2,3},{3,4},{4,5},{5,6},{6,7},{7,8},{8,9},{9,10},{10,1... | collective-permute-start | bytes 884744 | tf_op jit(solution)/shard_map/ppermute | solution.py:22
  31.6 1.3 %collective-permute-start.4 = (bf16[3,384,128]{2,1,0:T(8,128)(2,1)S(1)}, bf16[3,384,128]{2,1,0:T(8,128)(2,1)S(1)}, u32[]{:S(2)}, u32[]{:S(2)}) collective-permute-start(bf16[3,384,128]{2,1,0:T(8,128)(2,1)S(1)} %get-tuple-element.19), channel_id=1, source_target_pairs={{1,0},{2,1},{3,2},{4,3},{5,4},{6,5},{7,6},{8,7},{9,8},{10,9},{11,1... | collective-permute-start | bytes 884744 | tf_op jit(solution)/shard_map/ppermute | solution.py:22
  32.9 5.9 %collective-permute-done.3.from_left_ref.left_ref = bf16[3,384,128]{2,1,0:T(8,128)(2,1)S(1)} collective-permute-done((bf16[3,384,128]{2,1,0:T(8,128)(2,1)S(1)}, bf16[3,384,128]{2,1,0:T(8,128)(2,1)S(1)}, u32[]{:S(2)}, u32[]{:S(2)}) %collective-permute-start.3) | collective-permute-done | bytes 294944 | tf_op jit(solution)/shard_map/ppermute | solution.py:22
  38.8 4.4 %collective-permute-done.4.from_right_ref.right_ref = bf16[3,384,128]{2,1,0:T(8,128)(2,1)S(1)} collective-permute-done((bf16[3,384,128]{2,1,0:T(8,128)(2,1)S(1)}, bf16[3,384,128]{2,1,0:T(8,128)(2,1)S(1)}, u32[]{:S(2)}, u32[]{:S(2)}) %collective-permute-start.4) | collective-permute-done | bytes 294944 | tf_op jit(solution)/shard_map/ppermute | solution.py:22
  43.4 1.9 %collective-permute-start.5 = (bf16[3,3,128,128]{3,2,1,0:T(8,128)(2,1)S(1)}, bf16[3,3,128,128]{3,2,1,0:T(8,128)(2,1)S(1)}, u32[]{:S(2)}, u32[]{:S(2)}) collective-permute-start(bf16[3,3,128,128]{3,2,1,0:T(8,128)(2,1)S(1)} %get-tuple-element.20), channel_id=1, source_target_pairs={{0,32},{32,64},{64,96},{96,128},{128,160},{160,192},{192,224},{224... | collective-permute-start | bytes 884744 | tf_op jit(solution)/shard_map/ppermute | solution.py:22
  45.3 5.8 %collective-permute-start.6 = (bf16[3,3,128,128]{3,2,1,0:T(8,128)(2,1)S(1)}, bf16[3,3,128,128]{3,2,1,0:T(8,128)(2,1)S(1)}, u32[]{:S(2)}, u32[]{:S(2)}) collective-permute-start(bf16[3,3,128,128]{3,2,1,0:T(8,128)(2,1)S(1)} %get-tuple-element.21), channel_id=1, source_target_pairs={{32,0},{64,32},{96,64},{128,96},{160,128},{192,160},{224,192},{256... | collective-permute-start | bytes 884744 | tf_op jit(solution)/shard_map/ppermute | solution.py:22
  51.1 2.5 %collective-permute-done.5.above_ref = bf16[3,3,128,128]{3,2,1,0:T(8,128)(2,1)S(1)} collective-permute-done((bf16[3,3,128,128]{3,2,1,0:T(8,128)(2,1)S(1)}, bf16[3,3,128,128]{3,2,1,0:T(8,128)(2,1)S(1)}, u32[]{:S(2)}, u32[]{:S(2)}) %collective-permute-start.5) | collective-permute-done | bytes 294944 | tf_op jit(solution)/shard_map/ppermute | solution.py:22
  53.5 1.8 %collective-permute-done.6.below_ref = bf16[3,3,128,128]{3,2,1,0:T(8,128)(2,1)S(1)} collective-permute-done((bf16[3,3,128,128]{3,2,1,0:T(8,128)(2,1)S(1)}, bf16[3,3,128,128]{3,2,1,0:T(8,128)(2,1)S(1)}, u32[]{:S(2)}, u32[]{:S(2)}) %collective-permute-start.6) | collective-permute-done | bytes 294944 | tf_op jit(solution)/shard_map/ppermute | solution.py:22
  55.3 2.9 %shard_map.70 = (f32[2,3,384,128]{3,2,1,0:T(8,128)S(1)}, f32[2,256,128]{2,1,0:T(8,128)S(1)}, f32[2,3,384,128]{3,2,1,0:T(8,128)S(1)}, bf16[2,384,128]{2,1,0:T(8,128)(2,1)S(1)}, f32[2,128,128]{2,1,0:T(8,128)S(1)}) custom-call(s32[1,1]{1,0:T(1,128)S(6)} %copy.7.live_ref, s32[2,16]{1,0:T(2,128)S(1)} %bitcast.17, ...), custom_call_target="tpu_custom_call" | custom-call | flops 1000000000 | bytes 1000000 | tf_op jit(solution)/shard_map/pallas_call | solution.py:292
  58.2 10.5 %all_to_all.15 = bf16[16,16,128]{2,1,0:T(8,128)(2,1)S(1)} all-to-all(bf16[16,16,128]{2,1,0:T(8,128)(2,1)S(1)} %bitcast.18), channel_id=1, replica_groups=mesh['row'=16,'col'=32] {'row'}, dimensions={0} | all-to-all | bytes 131072 | tf_op jit(solution)/shard_map/all_to_all | solution.py:247
  68.7 3.8 %collective-permute-start.7 = (bf16[2,384,128]{2,1,0:T(8,128)(2,1)S(1)}, bf16[2,384,128]{2,1,0:T(8,128)(2,1)S(1)}, u32[]{:S(2)}, u32[]{:S(2)}) collective-permute-start(bf16[2,384,128]{2,1,0:T(8,128)(2,1)S(1)} %get-tuple-element.28), channel_id=1, source_target_pairs={{0,1},{1,2},{2,3},{3,4},{4,5},{5,6},{6,7},{7,8},{8,9},{9,10},{10,1... | collective-permute-start | bytes 589832 | tf_op jit(solution)/shard_map/ppermute | solution.py:22
  73.2 15.3 %all-to-all-start.1 = ((bf16[32,16,128]{2,1,0:T(8,128)(2,1)}), bf16[32,16,128]{2,1,0:T(8,128)(2,1)S(1)}, u32[]{:S(2)}, u32[]{:S(2)}) async-start(bf16[32,16,128]{2,1,0:T(8,128)(2,1)} %broadcast_in_dim.4), calls=%async_computation.1 | async-start | bytes 262144 | tf_op jit(solution)/shard_map/all_to_all | solution.py:247
  88.5 12.7 %all-to-all-done.1 = bf16[32,16,128]{2,1,0:T(8,128)(2,1)S(1)} async-done(((bf16[32,16,128]{2,1,0:T(8,128)(2,1)}), bf16[32,16,128]{2,1,0:T(8,128)(2,1)S(1)}, u32[]{:S(2)}, u32[]{:S(2)}) %all-to-all-start.1) | async-done | bytes 131104 | tf_op jit(solution)/shard_map/all_to_all | solution.py:247
  101.9 4.6 %all-to-all-start.2 = ((f32[16,16,128]{2,1,0:T(8,128)}), f32[16,16,128]{2,1,0:T(8,128)S(1)}, u32[]{:S(2)}, u32[]{:S(2)}) async-start(f32[16,16,128]{2,1,0:T(8,128)} %broadcast_in_dim.5), calls=%async_computation.2 | async-start | bytes 262144 | tf_op jit(solution)/shard_map/all_to_all | solution.py:247
  106.6 2.0 %collective-permute-start.8 = (bf16[2,2,128,128]{3,2,1,0:T(8,128)(2,1)S(1)}, bf16[2,2,128,128]{3,2,1,0:T(8,128)(2,1)S(1)}, u32[]{:S(2)}, u32[]{:S(2)}) collective-permute-start(bf16[2,2,128,128]{3,2,1,0:T(8,128)(2,1)S(1)} %pad_maximum_fusion.5), channel_id=1, source_target_pairs={{0,32},{32,64},{64,96},{96,128},{128,160},{160,192},{192,224},{224... | collective-permute-start | bytes 393224 | tf_op jit(solution)/shard_map/ppermute | solution.py:22
  108.6 6.4 %collective-permute-done.8.above_ref = bf16[2,2,128,128]{3,2,1,0:T(8,128)(2,1)S(1)} collective-permute-done((bf16[2,2,128,128]{3,2,1,0:T(8,128)(2,1)S(1)}, bf16[2,2,128,128]{3,2,1,0:T(8,128)(2,1)S(1)}, u32[]{:S(2)}, u32[]{:S(2)}) %collective-permute-start.8) | collective-permute-done | bytes 131104 | tf_op jit(solution)/shard_map/ppermute | solution.py:22
  115.0 0.9 shard_map.71
  115.9 0.8 shard_map.72
  (28 shorter events, 2.2 us)
Async XLA Ops:
  0.6 24.8 %copy-start.2 = (f32[2,256,256]{2,1,0:T(8,128)S(1)}, f32[2,256,256]{2,1,0:T(8,128)}, u32[]{:S(2)}) copy-start(f32[2,256,256]{2,1,0:T(8,128)} %obj_ref.1) | copy-start | bytes 1572868
  0.6 24.8 %copy-start.1 = (f32[2,128,128]{2,1,0:T(8,128)S(1)}, f32[2,128,128]{2,1,0:T(8,128)}, u32[]{:S(2)}) copy-start(f32[2,128,128]{2,1,0:T(8,128)} %probe_ref.5) | copy-start | bytes 393220
  0.7 24.8 %copy-start.3 = (s32[2,1,1,16]{3,2,1,0:T(1,128)S(1)}, s32[2,1,1,16]{3,2,1,0:T(1,128)}, u32[]{:S(2)}) copy-start(s32[2,1,1,16]{3,2,1,0:T(1,128)} %param.8) | copy-start | bytes 388
  0.7 24.8 %copy-start = (bf16[1,1,16,128,128]{4,3,2,1,0:T(8,128)(2,1)S(1)}, bf16[1,1,16,128,128]{4,3,2,1,0:T(8,128)(2,1)}, u32[]{:S(2)}) copy-start(bf16[1,1,16,128,128]{4,3,2,1,0:T(8,128)(2,1)} %param.7) | copy-start | bytes 1572868
  1.8 21.3 %collective-permute-start.2 = (bf16[2,128,128]{2,1,0:T(8,128)(2,1)S(1)}, bf16[2,128,128]{2,1,0:T(8,128)(2,1)S(1)}, u32[]{:S(2)}, u32[]{:S(2)}) collective-permute-start(bf16[2,128,128]{2,1,0:T(8,128)(2,1)S(1)} %slice.33), channel_id=1, source_target_pairs={{33,0},{34,1},{35,2},{36,3},{37,4},{38,5},{39,6},{40,7},{41,8},{42... | collective-permute-start | bytes 196616 | tf_op jit(solution)/shard_map/ppermute | solution.py:22
  18.6 6.9 %collective-permute-start = (bf16[2,256,128]{2,1,0:T(8,128)(2,1)S(1)}, bf16[2,256,128]{2,1,0:T(8,128)(2,1)S(1)}, u32[]{:S(2)}, u32[]{:S(2)}) collective-permute-start(bf16[2,256,128]{2,1,0:T(8,128)(2,1)S(1)} %slice.31), channel_id=1, source_target_pairs={{1,0},{2,1},{3,2},{4,3},{5,4},{6,5},{7,6},{8,7},{9,8},{10,9},{11,1... | collective-permute-start | bytes 393224 | tf_op jit(solution)/shard_map/ppermute | solution.py:22
  19.9 5.5 %collective-permute-start.1 = (bf16[2,128,256]{2,1,0:T(8,128)(2,1)S(1)}, bf16[2,128,256]{2,1,0:T(8,128)(2,1)S(1)}, u32[]{:S(2)}, u32[]{:S(2)}) collective-permute-start(bf16[2,128,256]{2,1,0:T(8,128)(2,1)S(1)} %slice.32), channel_id=1, source_target_pairs={{32,0},{64,32},{96,64},{128,96},{160,128},{192,160},{224,192},{256... | collective-permute-start | bytes 393224 | tf_op jit(solution)/shard_map/ppermute | solution.py:22
  28.2 10.7 %collective-permute-start.3 = (bf16[3,384,128]{2,1,0:T(8,128)(2,1)S(1)}, bf16[3,384,128]{2,1,0:T(8,128)(2,1)S(1)}, u32[]{:S(2)}, u32[]{:S(2)}) collective-permute-start(bf16[3,384,128]{2,1,0:T(8,128)(2,1)S(1)} %get-tuple-element.18), channel_id=1, source_target_pairs={{0,1},{1,2},{2,3},{3,4},{4,5},{5,6},{6,7},{7,8},{8,9},{9,10},{10,1... | collective-permute-start | bytes 884744 | tf_op jit(solution)/shard_map/ppermute | solution.py:22
  31.6 11.7 %collective-permute-start.4 = (bf16[3,384,128]{2,1,0:T(8,128)(2,1)S(1)}, bf16[3,384,128]{2,1,0:T(8,128)(2,1)S(1)}, u32[]{:S(2)}, u32[]{:S(2)}) collective-permute-start(bf16[3,384,128]{2,1,0:T(8,128)(2,1)S(1)} %get-tuple-element.19), channel_id=1, source_target_pairs={{1,0},{2,1},{3,2},{4,3},{5,4},{6,5},{7,6},{8,7},{9,8},{10,9},{11,1... | collective-permute-start | bytes 884744 | tf_op jit(solution)/shard_map/ppermute | solution.py:22
  43.4 10.2 %collective-permute-start.5 = (bf16[3,3,128,128]{3,2,1,0:T(8,128)(2,1)S(1)}, bf16[3,3,128,128]{3,2,1,0:T(8,128)(2,1)S(1)}, u32[]{:S(2)}, u32[]{:S(2)}) collective-permute-start(bf16[3,3,128,128]{3,2,1,0:T(8,128)(2,1)S(1)} %get-tuple-element.20), channel_id=1, source_target_pairs={{0,32},{32,64},{64,96},{96,128},{128,160},{160,192},{192,224},{224... | collective-permute-start | bytes 884744 | tf_op jit(solution)/shard_map/ppermute | solution.py:22
  45.3 10.0 %collective-permute-start.6 = (bf16[3,3,128,128]{3,2,1,0:T(8,128)(2,1)S(1)}, bf16[3,3,128,128]{3,2,1,0:T(8,128)(2,1)S(1)}, u32[]{:S(2)}, u32[]{:S(2)}) collective-permute-start(bf16[3,3,128,128]{3,2,1,0:T(8,128)(2,1)S(1)} %get-tuple-element.21), channel_id=1, source_target_pairs={{32,0},{64,32},{96,64},{128,96},{160,128},{192,160},{224,192},{256... | collective-permute-start | bytes 884744 | tf_op jit(solution)/shard_map/ppermute | solution.py:22
  68.7 19.8 %collective-permute-start.7 = (bf16[2,384,128]{2,1,0:T(8,128)(2,1)S(1)}, bf16[2,384,128]{2,1,0:T(8,128)(2,1)S(1)}, u32[]{:S(2)}, u32[]{:S(2)}) collective-permute-start(bf16[2,384,128]{2,1,0:T(8,128)(2,1)S(1)} %get-tuple-element.28), channel_id=1, source_target_pairs={{0,1},{1,2},{2,3},{3,4},{4,5},{5,6},{6,7},{7,8},{8,9},{9,10},{10,1... | collective-permute-start | bytes 589832 | tf_op jit(solution)/shard_map/ppermute | solution.py:22
  73.2 28.1 %all-to-all-start.1 = ((bf16[32,16,128]{2,1,0:T(8,128)(2,1)}), bf16[32,16,128]{2,1,0:T(8,128)(2,1)S(1)}, u32[]{:S(2)}, u32[]{:S(2)}) async-start(bf16[32,16,128]{2,1,0:T(8,128)(2,1)} %broadcast_in_dim.4), calls=%async_computation.1 | async-start | bytes 262144 | tf_op jit(solution)/shard_map/all_to_all | solution.py:247
  101.9 13.9 %all-to-all-start.2 = ((f32[16,16,128]{2,1,0:T(8,128)}), f32[16,16,128]{2,1,0:T(8,128)S(1)}, u32[]{:S(2)}, u32[]{:S(2)}) async-start(f32[16,16,128]{2,1,0:T(8,128)} %broadcast_in_dim.5), calls=%async_computation.2 | async-start | bytes 262144 | tf_op jit(solution)/shard_map/all_to_all | solution.py:247
  106.6 8.4 %collective-permute-start.8 = (bf16[2,2,128,128]{3,2,1,0:T(8,128)(2,1)S(1)}, bf16[2,2,128,128]{3,2,1,0:T(8,128)(2,1)S(1)}, u32[]{:S(2)}, u32[]{:S(2)}) collective-permute-start(bf16[2,2,128,128]{3,2,1,0:T(8,128)(2,1)S(1)} %pad_maximum_fusion.5), channel_id=1, source_target_pairs={{0,32},{32,64},{64,96},{96,128},{128,160},{160,192},{192,224},{224... | collective-permute-start | bytes 393224 | tf_op jit(solution)/shard_map/ppermute | solution.py:22
where the time goes:
time: 117 us
  starting transfers between devices  58.1 us (50%)
  waiting for transfers between devices  35.9 us (31%)
  blocking collectives  10.5 us (9%)
  Pallas kernels  7.36 us (6%)
  other arithmetic  1.86 us (2%)
  between operations  1.53 us (1%)
  local copies, waits for them, and re-layouts  1.39 us (1%)
    ppermute x9, starting transfers between devices, shift(): lax.ppermute(value, axis, [(source, source + steps) for source in range(f...  38.2 us
    ppermute x9, waiting for transfers between devices, shift(): lax.ppermute(value, axis, [(source, source + steps) for source in range(f...  23.3 us
    all_to_all x2, starting transfers between devices, exchange(): return lax.all_to_all(parts, axis, 0, 0, tiled=True)  20 us
    all_to_all x2, waiting for transfers between devices, exchange(): return lax.all_to_all(parts, axis, 0, 0, tiled=True)  12.7 us
    all_to_all x1, blocking collectives, exchange(): return lax.all_to_all(parts, axis, 0, 0, tiled=True)  10.5 us
    pallas_call x1, Pallas kernels, sweeps(): call(second_kernel, [((2, 3, wide, window), F32), ((2, tile, window), F32...  2.86 us
    pallas_call x1, Pallas kernels, sweeps(): call(first_kernel, [((2, 3, wide, window), F32), ((3, 3, wide, window), F...  2.69 us
  transfers between devices with their start and end apart: 11, of which 7 were waited for; matrix products, arithmetic and copies ran while one was open for 1% of the time, Pallas kernels for 1%

commit v1 on v0

--- a/solution.py
+++ b/solution.py
@@ -49,7 +49,7 @@
 
 def sweep_slots(
     live_ref, corners_ref, ext_ref, probe_ref, amp_ref, tab_ref,
-    dep_ref, grad_ref, power_ref, patch_ref, wave_ref, with_light,
+    dep_ref, grad_ref, patch_ref, wave_ref,
 ):
     window = probe_ref.shape[1]
     live = live_ref[0, 0]
@@ -76,7 +76,7 @@
                 near = pltpu.roll(ext_ref[part, block, rows, :], back, 1)
                 far = pltpu.roll(ext_ref[part, block + 1, rows, :], back, 1)
                 pieces.append(jnp.where(inside, near, far))
-            if not with_light:
+            if grad_ref is not None:
                 patch_ref[member, 0] = pieces[0]
                 patch_ref[member, 1] = pieces[1]
             pr, pi = probe_ref[0], probe_ref[1]
@@ -119,9 +119,7 @@
                 pr, pi = probe_ref[0], probe_ref[1]
                 accumulate(dep_ref, 0, block, row, turn, lanes, pr * cr + pi * ci)
                 accumulate(dep_ref, 1, block, row, turn, lanes, pr * ci - pi * cr)
-                if with_light:
-                    accumulate(dep_ref, 2, block, row, turn, lanes, power_ref[...] * weight)
-                else:
+                if grad_ref is not None:
                     xr, xi = patch_ref[m, 0], patch_ref[m, 1]
                     grad_ref[0] += xr * cr + xi * ci
                     grad_ref[1] += xr * ci - xi * cr
@@ -130,9 +128,35 @@
     lax.fori_loop(0, (live + GROUP - 1) // GROUP, step, 0)
 
 
+def light_kernel(
+    live_ref, corners_ref, probe_ref, light_ref, to_right_ref, to_left_ref, power_ref
+):
+    window = probe_ref.shape[1]
+    live = live_ref[0, 0]
+    lanes = lax.broadcasted_iota(jnp.int32, (window, window), 1)
+    light_ref[...] = jnp.zeros(light_ref.shape, F32)
+    power_ref[...] = probe_ref[0] * probe_ref[0] + probe_ref[1] * probe_ref[1]
+
+    def step(index, carry):
+        for member in range(4):
+            slot = index * 4 + member
+            weight = jnp.where(slot < live, 1.0, 0.0).astype(F32)
+            row = corners_ref[0, slot]
+            col = corners_ref[1, slot]
+            block = col // window
+            accumulate(
+                light_ref, 0, block, row, col - block * window, lanes, power_ref[...] * weight
+            )
+        return carry
+
+    lax.fori_loop(0, (live + 3) // 4, step, 0)
+    to_right_ref[0] = light_ref[0, 2].astype(TERMS)
+    to_left_ref[0] = light_ref[0, 0].astype(TERMS)
+
+
 def first_kernel(
     live_ref, corners_ref, obj_ref, right_ref, low_ref, corner_ref, probe_ref, amp_ref, tab_ref,
-    ext_ref, dep_ref, to_right_ref, to_left_ref, power_ref, patch_ref, wave_ref,
+    ext_ref, dep_ref, to_right_ref, to_left_ref, patch_ref, wave_ref,
 ):
     window = probe_ref.shape[1]
     tile = obj_ref.shape[1]
@@ -144,30 +168,35 @@
         ext_ref[part, 2, 0:tile, :] = right_ref[part].astype(F32)
         ext_ref[part, 2, tile:, :] = corner_ref[part].astype(F32)
     dep_ref[...] = jnp.zeros(dep_ref.shape, F32)
-    power_ref[...] = probe_ref[0] * probe_ref[0] + probe_ref[1] * probe_ref[1]
     sweep_slots(
         live_ref, corners_ref, ext_ref, probe_ref, amp_ref, tab_ref,
-        dep_ref, None, power_ref, patch_ref, wave_ref, True,
-    )
-    for part in range(3):
+        dep_ref, None, patch_ref, wave_ref,
+    )
+    for part in range(2):
         to_right_ref[part] = dep_ref[part, 2].astype(TERMS)
         to_left_ref[part] = dep_ref[part, 0].astype(TERMS)
 
 
-def middle_kernel(dep_ref, from_left_ref, from_right_ref, down_ref, up_ref):
+def middle_kernel(
+    dep_ref, light_ref, from_left_ref, from_right_ref, light_left_ref, light_right_ref,
+    down_ref, up_ref,
+):
     window = from_left_ref.shape[2]
     tile = from_left_ref.shape[1] - window
-    for part in range(3):
+    sources = [(dep_ref, from_left_ref, from_right_ref, part, part) for part in range(2)]
+    sources.append((light_ref, light_left_ref, light_right_ref, 0, 2))
+    for own, left, right, part, place in sources:
         for ref, rows in ((down_ref, slice(tile, tile + window)), (up_ref, slice(0, window))):
-            ref[part, 0] = (dep_ref[part, 0, rows, :] + from_left_ref[part, rows, :].astype(F32)).astype(TERMS)
-            ref[part, 1] = dep_ref[part, 1, rows, :].astype(TERMS)
-            ref[part, 2] = (dep_ref[part, 2, rows, :] + from_right_ref[part, rows, :].astype(F32)).astype(TERMS)
+            ref[place, 0] = (own[part, 0, rows, :] + left[part, rows, :].astype(F32)).astype(TERMS)
+            ref[place, 1] = own[part, 1, rows, :].astype(TERMS)
+            ref[place, 2] = (own[part, 2, rows, :] + right[part, rows, :].astype(F32)).astype(TERMS)
 
 
 def second_kernel(
-    live_ref, corners_ref, ext_ref, dep_in_ref, left_ref, right_ref, above_ref, below_ref,
+    live_ref, corners_ref, ext_ref, dep_in_ref, light_ref, left_ref, right_ref,
+    light_left_ref, light_right_ref, above_ref, below_ref,
     probe_ref, amp_ref, tab_ref,
-    upd_ref, den_ref, dep_ref, to_right_ref, grad_ref, sum_ref, patch_ref, wave_ref,
+    upd_ref, den_ref, dep_ref, to_right_ref, grad_ref, patch_ref, wave_ref,
 ):
     window = probe_ref.shape[1]
     total = ext_ref.shape[2]
@@ -177,11 +206,14 @@
             rows = slice(first, first + window)
             sums = []
             for part in (2, 0, 1):
-                value = dep_in_ref[part, block, rows, :]
+                own, left, right, place = dep_in_ref, left_ref, right_ref, part
+                if part == 2:
+                    own, left, right, place = light_ref, light_left_ref, light_right_ref, 0
+                value = own[place, block, rows, :]
                 if block == 0:
-                    value = value + left_ref[part, rows, :].astype(F32)
+                    value = value + left[place, rows, :].astype(F32)
                 if block == 2:
-                    value = value + right_ref[part, rows, :].astype(F32)
+                    value = value + right[place, rows, :].astype(F32)
                 if first == 0:
                     value = value + above_ref[part, block].astype(F32)
                 if first == tile:
@@ -196,7 +228,7 @@
     grad_ref[...] = jnp.zeros(grad_ref.shape, F32)
     sweep_slots(
         live_ref, corners_ref, upd_ref, probe_ref, amp_ref, tab_ref,
-        dep_ref, grad_ref, None, patch_ref, wave_ref, False,
+        dep_ref, grad_ref, patch_ref, wave_ref,
     )
     for part in range(2):
         to_right_ref[part] = dep_ref[part, 2].astype(TERMS)
@@ -252,29 +284,37 @@
     window = probe.shape[1]
     tile = object_field.shape[1]
     wide = tile + window
-    across = lax.axis_size("col")
+
     amp = amplitude.reshape(slots, window, window)
     spots = corners.reshape(2, slots)
     live = live_count.reshape(1, 1)
     tables = dft_tables(window)
 
+    diagonal = shift(
+        object_field[:, :window, :window].astype(HALO), ("row", "col"), -(lax.axis_size("col") + 1)
+    )
     right = shift(object_field[:, :, :window].astype(HALO), "col", -1)
     low = shift(object_field[:, :window, :].astype(HALO), "row", -1)
-    diagonal = shift(
-        object_field[:, :window, :window].astype(HALO), ("row", "col"), -(across + 1)
-    )
+    strip = (wide, window)
+    light, light_right, light_left = call(
+        light_kernel,
+        [((1, 3) + strip, F32), ((1,) + strip, TERMS), ((1,) + strip, TERMS)],
+        [SM, SM, VM],
+        [pltpu.VMEM((window, window), F32)],
+    )(live, spots, probe)
+    light_from_left = shift(light_right, "col", 1)
+    light_from_right = shift(light_left, "col", -1)
     scratch = [
-        pltpu.VMEM((window, window), F32),
         pltpu.VMEM((GROUP, 2, window, window), F32),
         pltpu.VMEM((GROUP, window, 2 * window), BF16),
     ]
     ext, dep, to_right, to_left = call(
         first_kernel,
         [
-            ((2, 3, wide, window), F32),
-            ((3, 3, wide, window), F32),
-            ((3, wide, window), TERMS),
-            ((3, wide, window), TERMS),
+            ((2, 3) + strip, F32),
+            ((2, 3) + strip, F32),
+            ((2,) + strip, TERMS),
+            ((2,) + strip, TERMS),
         ],
         [SM, SM] + [VM] * 7,
         scratch,
@@ -284,8 +324,8 @@
     from_left = shift(to_right, "col", 1)
     from_right = shift(to_left, "col", -1)
     down, up = call(
-        middle_kernel, [((3, 3, window, window), TERMS), ((3, 3, window, window), TERMS)], [VM] * 3
-    )(dep, from_left, from_right)
+        middle_kernel, [((3, 3, window, window), TERMS), ((3, 3, window, window), TERMS)], [VM] * 6
+    )(dep, light, from_left, from_right, light_from_left, light_from_right)
     from_above = shift(down, "row", 1)
     from_below = shift(up, "row", -1)
 
@@ -298,28 +338,31 @@
             ((2, wide, window), TERMS),
             ((2, window, window), F32),
         ],
-        [SM, SM] + [VM] * 9,
+        [SM, SM] + [VM] * 12,
         scratch,
         10**9,
-    )(live, spots, ext, dep, from_left, from_right, from_above, from_below, probe, amp, tables)
+    )(
+        live, spots, ext, dep, light, from_left, from_right, light_from_left, light_from_right,
+        from_above, from_below, probe, amp, tables,
+    )
 
     rows, cols = lax.axis_size("row"), lax.axis_size("col")
     parts = exchange(gradient.astype(GRAD).reshape(rows, -1, window), "row")
     part = jnp.sum(parts.astype(F32), 0).astype(GRAD)
-    to_right, dep, ignored = lax.optimization_barrier((to_right, dep, part))
+    to_right, dep, _ = lax.optimization_barrier((to_right, dep, part))
     parts = exchange(jnp.broadcast_to(part[None], (cols,) + part.shape), "col")
     from_left = shift(to_right, "col", 1)
     spill = dep[:, :2, tile:, :]
     spill = jnp.concatenate(
         [(spill[:, :1] + from_left[:, None, tile:].astype(F32)), spill[:, 1:]], 1
     ).astype(TERMS)
-    part = jnp.sum(parts.astype(F32), 0)
-    spill, ignored = lax.optimization_barrier((spill, part))
-    parts = exchange(jnp.broadcast_to(part[None], (rows,) + part.shape), "row")
     from_above = shift(spill, "row", 1)
     refined = call(
         finish_kernel, [((2, tile, tile), F32)], [VM] * 5
     )(updated, inverse, dep, from_left, from_above)[0]
+    parts, refined = lax.optimization_barrier((parts, refined))
+    part = jnp.sum(parts.astype(F32), 0)
+    parts = exchange(jnp.broadcast_to(part[None], (rows,) + part.shape), "row")
     new_probe = call(probe_kernel, [(probe.shape, F32)], [VM] * 2)(
         probe, parts.reshape(gradient.shape)
     )[0]

time: 117 us -> 117 us (level)
  the two profiles are of different devices: /device:TPU:8 before, /device:TPU:1 now
where the time goes in v1:
time: 117 us; the launch traced here: 116 us
  starting transfers between devices  51.8 us (44%)
  waiting for transfers between devices  28.1 us (24%)
  blocking collectives  24.1 us (21%)
  Pallas kernels  8.03 us (7%)
  other arithmetic  1.86 us (2%)
  between operations  1.56 us (1%)
    ppermute x11, starting transfers between devices, shift(): lax.ppermute(value, axis, [(source, source + steps) for source in range(f...  35.7 us
    all_to_all x2, blocking collectives, exchange(): return lax.all_to_all(parts, axis, 0, 0, tiled=True)  24.1 us
    ppermute x11, waiting for transfers between devices, shift(): lax.ppermute(value, axis, [(source, source + steps) for source in range(f...  22.5 us
    all_to_all x1, starting transfers between devices, exchange(): return lax.all_to_all(parts, axis, 0, 0, tiled=True)  16.1 us
    all_to_all x1, waiting for transfers between devices, exchange(): return lax.all_to_all(parts, axis, 0, 0, tiled=True)  5.54 us
    pallas_call x1, Pallas kernels, sweeps(): call(second_kernel, [((2, 3, wide, window), F32), ((2, tile, window), F32...  2.85 us
    pallas_call x1, Pallas kernels, sweeps(): call(first_kernel, [((2, 3) + strip, F32), ((2, 3) + strip, F32), ((2,) +...  2.47 us
  transfers between devices with their start and end apart: 12, of which 8 were waited for; matrix products, arithmetic and copies ran while one was open for 1% of the time, Pallas kernels for 2%

profile of v1, /device:TPU:1, one launch (start us, length us, event | category | flops | bytes accessed | tf_op | source)
XLA Modules:
  0.0 116.3 jit_solution(14440612438648930385)
XLA Ops:
  0.7 1.2 convert.46
  1.8 1.3 %collective-permute-start.2 = (bf16[2,128,128]{2,1,0:T(8,128)(2,1)S(1)}, bf16[2,128,128]{2,1,0:T(8,128)(2,1)S(1)}, u32[]{:S(2)}, u32[]{:S(2)}) collective-permute-start(bf16[2,128,128]{2,1,0:T(8,128)(2,1)S(1)} %slice.33), channel_id=1, source_target_pairs={{33,0},{34,1},{35,2},{36,3},{37,4},{38,5},{39,6},{40,7},{41,8},{42... | collective-permute-start | bytes 196616 | tf_op jit(solution)/shard_map/ppermute | solution.py:22
  3.2 1.3 %collective-permute-start = (bf16[2,256,128]{2,1,0:T(8,128)(2,1)S(1)}, bf16[2,256,128]{2,1,0:T(8,128)(2,1)S(1)}, u32[]{:S(2)}, u32[]{:S(2)}) collective-permute-start(bf16[2,256,128]{2,1,0:T(8,128)(2,1)S(1)} %slice.31), channel_id=1, source_target_pairs={{1,0},{2,1},{3,2},{4,3},{5,4},{6,5},{7,6},{8,7},{9,8},{10,9},{11,1... | collective-permute-start | bytes 393224 | tf_op jit(solution)/shard_map/ppermute | solution.py:22
  4.5 8.7 %collective-permute-start.1 = (bf16[2,128,256]{2,1,0:T(8,128)(2,1)S(1)}, bf16[2,128,256]{2,1,0:T(8,128)(2,1)S(1)}, u32[]{:S(2)}, u32[]{:S(2)}) collective-permute-start(bf16[2,128,256]{2,1,0:T(8,128)(2,1)S(1)} %slice.32), channel_id=1, source_target_pairs={{32,0},{64,32},{96,64},{128,96},{160,128},{192,160},{224,192},{256... | collective-permute-start | bytes 393224 | tf_op jit(solution)/shard_map/ppermute | solution.py:22
  14.5 3.3 %collective-permute-done.right_ref = bf16[2,256,128]{2,1,0:T(8,128)(2,1)S(1)} collective-permute-done((bf16[2,256,128]{2,1,0:T(8,128)(2,1)S(1)}, bf16[2,256,128]{2,1,0:T(8,128)(2,1)S(1)}, u32[]{:S(2)}, u32[]{:S(2)}) %collective-permute-start) | collective-permute-done | bytes 131104 | tf_op jit(solution)/shard_map/ppermute | solution.py:22
  17.8 7.1 %collective-permute-done.1.low_ref = bf16[2,128,256]{2,1,0:T(8,128)(2,1)S(1)} collective-permute-done((bf16[2,128,256]{2,1,0:T(8,128)(2,1)S(1)}, bf16[2,128,256]{2,1,0:T(8,128)(2,1)S(1)}, u32[]{:S(2)}, u32[]{:S(2)}) %collective-permute-start.1) | collective-permute-done | bytes 131104 | tf_op jit(solution)/shard_map/ppermute | solution.py:22
  25.0 2.5 %shard_map.68 = (f32[2,3,384,128]{3,2,1,0:T(8,128)S(1)}, f32[2,3,384,128]{3,2,1,0:T(8,128)S(1)}, bf16[2,384,128]{2,1,0:T(8,128)(2,1)S(1)}, bf16[2,384,128]{2,1,0:T(8,128)(2,1)S(1)}) custom-call(s32[1,1]{1,0:T(1,128)S(6)} %copy.7.live_ref, s32[2,16]{1,0:T(2,128)S(1)} %bitcast.16, f32[2,256,256]{2,1,0:T(8,128)S(1)} %copy-done.2, ...), custom_call_target="tpu_custom_call" | custom-call | flops 1000000000 | bytes 1000000 | tf_op jit(solution)/shard_map/pallas_call | solution.py:311
  27.4 6.0 %collective-permute-start.3 = (bf16[2,384,128]{2,1,0:T(8,128)(2,1)S(1)}, bf16[2,384,128]{2,1,0:T(8,128)(2,1)S(1)}, u32[]{:S(2)}, u32[]{:S(2)}) collective-permute-start(bf16[2,384,128]{2,1,0:T(8,128)(2,1)S(1)} %get-tuple-element.23), channel_id=1, source_target_pairs={{0,1},{1,2},{2,3},{3,4},{4,5},{5,6},{6,7},{7,8},{8,9},{9,10},{10,1... | collective-permute-start | bytes 589832 | tf_op jit(solution)/shard_map/ppermute | solution.py:22
  33.4 1.3 %collective-permute-start.4 = (bf16[2,384,128]{2,1,0:T(8,128)(2,1)S(1)}, bf16[2,384,128]{2,1,0:T(8,128)(2,1)S(1)}, u32[]{:S(2)}, u32[]{:S(2)}) collective-permute-start(bf16[2,384,128]{2,1,0:T(8,128)(2,1)S(1)} %get-tuple-element.24), channel_id=1, source_target_pairs={{1,0},{2,1},{3,2},{4,3},{5,4},{6,5},{7,6},{8,7},{9,8},{10,9},{11,1... | collective-permute-start | bytes 589832 | tf_op jit(solution)/shard_map/ppermute | solution.py:22
  35.6 4.3 %collective-permute-start.5 = (bf16[1,384,128]{2,1,0:T(8,128)(2,1)S(1)}, bf16[1,384,128]{2,1,0:T(8,128)(2,1)S(1)}, u32[]{:S(2)}, u32[]{:S(2)}) collective-permute-start(bf16[1,384,128]{2,1,0:T(8,128)(2,1)S(1)} %get-tuple-element.25), channel_id=1, source_target_pairs={{0,1},{1,2},{2,3},{3,4},{4,5},{5,6},{6,7},{7,8},{8,9},{9,10},{10,1... | collective-permute-start | bytes 294920 | tf_op jit(solution)/shard_map/ppermute | solution.py:22
  39.9 1.3 %collective-permute-start.6 = (bf16[1,384,128]{2,1,0:T(8,128)(2,1)S(1)}, bf16[1,384,128]{2,1,0:T(8,128)(2,1)S(1)}, u32[]{:S(2)}, u32[]{:S(2)}) collective-permute-start(bf16[1,384,128]{2,1,0:T(8,128)(2,1)S(1)} %get-tuple-element.26), channel_id=1, source_target_pairs={{1,0},{2,1},{3,2},{4,3},{5,4},{6,5},{7,6},{8,7},{9,8},{10,9},{11,1... | collective-permute-start | bytes 294920 | tf_op jit(solution)/shard_map/ppermute | solution.py:22
  41.6 3.7 %collective-permute-done.6.light_right_ref = bf16[1,384,128]{2,1,0:T(8,128)(2,1)S(1)} collective-permute-done((bf16[1,384,128]{2,1,0:T(8,128)(2,1)S(1)}, bf16[1,384,128]{2,1,0:T(8,128)(2,1)S(1)}, u32[]{:S(2)}, u32[]{:S(2)}) %collective-permute-start.6) | collective-permute-done | bytes 98336 | tf_op jit(solution)/shard_map/ppermute | solution.py:22
  45.4 2.8 %collective-permute-start.7 = (bf16[3,3,128,128]{3,2,1,0:T(8,128)(2,1)S(1)}, bf16[3,3,128,128]{3,2,1,0:T(8,128)(2,1)S(1)}, u32[]{:S(2)}, u32[]{:S(2)}) collective-permute-start(bf16[3,3,128,128]{3,2,1,0:T(8,128)(2,1)S(1)} %get-tuple-element.27), channel_id=1, source_target_pairs={{0,32},{32,64},{64,96},{96,128},{128,160},{160,192},{192,224},{224... | collective-permute-start | bytes 884744 | tf_op jit(solution)/shard_map/ppermute | solution.py:22
  48.2 1.9 %collective-permute-start.8 = (bf16[3,3,128,128]{3,2,1,0:T(8,128)(2,1)S(1)}, bf16[3,3,128,128]{3,2,1,0:T(8,128)(2,1)S(1)}, u32[]{:S(2)}, u32[]{:S(2)}) collective-permute-start(bf16[3,3,128,128]{3,2,1,0:T(8,128)(2,1)S(1)} %get-tuple-element.28), channel_id=1, source_target_pairs={{32,0},{64,32},{96,64},{128,96},{160,128},{192,160},{224,192},{256... | collective-permute-start | bytes 884744 | tf_op jit(solution)/shard_map/ppermute | solution.py:22
  50.1 1.7 %collective-permute-done.7.above_ref = bf16[3,3,128,128]{3,2,1,0:T(8,128)(2,1)S(1)} collective-permute-done((bf16[3,3,128,128]{3,2,1,0:T(8,128)(2,1)S(1)}, bf16[3,3,128,128]{3,2,1,0:T(8,128)(2,1)S(1)}, u32[]{:S(2)}, u32[]{:S(2)}) %collective-permute-start.7) | collective-permute-done | bytes 294944 | tf_op jit(solution)/shard_map/ppermute | solution.py:22
  51.8 4.4 %collective-permute-done.8.below_ref = bf16[3,3,128,128]{3,2,1,0:T(8,128)(2,1)S(1)} collective-permute-done((bf16[3,3,128,128]{3,2,1,0:T(8,128)(2,1)S(1)}, bf16[3,3,128,128]{3,2,1,0:T(8,128)(2,1)S(1)}, u32[]{:S(2)}, u32[]{:S(2)}) %collective-permute-start.8) | collective-permute-done | bytes 294944 | tf_op jit(solution)/shard_map/ppermute | solution.py:22
  56.2 2.8 %shard_map.71 = (f32[2,3,384,128]{3,2,1,0:T(8,128)S(1)}, f32[2,256,128]{2,1,0:T(8,128)S(1)}, f32[2,3,384,128]{3,2,1,0:T(8,128)S(1)}, bf16[2,384,128]{2,1,0:T(8,128)(2,1)S(1)}, f32[2,128,128]{2,1,0:T(8,128)S(1)}) custom-call(s32[1,1]{1,0:T(1,128)S(6)} %copy.7.live_ref, s32[2,16]{1,0:T(2,128)S(1)} %bitcast.18, ...), custom_call_target="tpu_custom_call" | custom-call | flops 1000000000 | bytes 1000000 | tf_op jit(solution)/shard_map/pallas_call | solution.py:332
  59.1 13.4 %all_to_all.15 = bf16[16,16,128]{2,1,0:T(8,128)(2,1)S(1)} all-to-all(bf16[16,16,128]{2,1,0:T(8,128)(2,1)S(1)} %bitcast.19), channel_id=1, replica_groups=mesh['row'=16,'col'=32] {'row'}, dimensions={0} | all-to-all | bytes 131072 | tf_op jit(solution)/shard_map/all_to_all | solution.py:279
  72.5 3.8 %collective-permute-start.9 = (bf16[2,384,128]{2,1,0:T(8,128)(2,1)S(1)}, bf16[2,384,128]{2,1,0:T(8,128)(2,1)S(1)}, u32[]{:S(2)}, u32[]{:S(2)}) collective-permute-start(bf16[2,384,128]{2,1,0:T(8,128)(2,1)S(1)} %get-tuple-element.35), channel_id=1, source_target_pairs={{0,1},{1,2},{2,3},{3,4},{4,5},{5,6},{6,7},{7,8},{8,9},{9,10},{10,1... | collective-permute-start | bytes 589832 | tf_op jit(solution)/shard_map/ppermute | solution.py:22
  77.0 16.1 %all-to-all-start.1 = ((bf16[32,16,128]{2,1,0:T(8,128)(2,1)}), bf16[32,16,128]{2,1,0:T(8,128)(2,1)S(1)}, u32[]{:S(2)}, u32[]{:S(2)}) async-start(bf16[32,16,128]{2,1,0:T(8,128)(2,1)} %broadcast_in_dim.4), calls=%async_computation.1 | async-start | bytes 262144 | tf_op jit(solution)/shard_map/all_to_all | solution.py:279
  93.2 3.0 %collective-permute-start.10 = (bf16[2,2,128,128]{3,2,1,0:T(8,128)(2,1)S(1)}, bf16[2,2,128,128]{3,2,1,0:T(8,128)(2,1)S(1)}, u32[]{:S(2)}, u32[]{:S(2)}) collective-permute-start(bf16[2,2,128,128]{3,2,1,0:T(8,128)(2,1)S(1)} %pad_maximum_fusion.5), channel_id=1, source_target_pairs={{0,32},{32,64},{64,96},{96,128},{128,160},{160,192},{192,224},{224... | collective-permute-start | bytes 393224 | tf_op jit(solution)/shard_map/ppermute | solution.py:22
  96.2 1.9 %collective-permute-done.10.above_ref = bf16[2,2,128,128]{3,2,1,0:T(8,128)(2,1)S(1)} collective-permute-done((bf16[2,2,128,128]{3,2,1,0:T(8,128)(2,1)S(1)}, bf16[2,2,128,128]{3,2,1,0:T(8,128)(2,1)S(1)}, u32[]{:S(2)}, u32[]{:S(2)}) %collective-permute-start.10) | collective-permute-done | bytes 131104 | tf_op jit(solution)/shard_map/ppermute | solution.py:22
  99.1 5.5 %all-to-all-done.1 = bf16[32,16,128]{2,1,0:T(8,128)(2,1)S(1)} async-done(((bf16[32,16,128]{2,1,0:T(8,128)(2,1)}), bf16[32,16,128]{2,1,0:T(8,128)(2,1)S(1)}, u32[]{:S(2)}, u32[]{:S(2)}) %all-to-all-start.1) | async-done | bytes 131104 | tf_op jit(solution)/shard_map/all_to_all | solution.py:279
  104.7 10.8 %all_to_all.16 = f32[16,16,128]{2,1,0:T(8,128)S(1)} all-to-all(f32[16,16,128]{2,1,0:T(8,128)S(1)} %broadcast_in_dim.5), channel_id=1, replica_groups=mesh['row'=16,'col'=32] {'row'}, dimensions={0} | all-to-all | bytes 262144 | tf_op jit(solution)/shard_map/all_to_all | solution.py:279
  (32 shorter events, 4.5 us)
Async XLA Ops:
  0.6 24.3 %copy-start.2 = (f32[2,256,256]{2,1,0:T(8,128)S(1)}, f32[2,256,256]{2,1,0:T(8,128)}, u32[]{:S(2)}) copy-start(f32[2,256,256]{2,1,0:T(8,128)} %obj_ref.1) | copy-start | bytes 1572868
  0.6 24.3 %copy-start = (f32[2,128,128]{2,1,0:T(8,128)S(1)}, f32[2,128,128]{2,1,0:T(8,128)}, u32[]{:S(2)}) copy-start(f32[2,128,128]{2,1,0:T(8,128)} %probe_ref.7) | copy-start | bytes 393220
  0.7 24.3 %copy-start.3 = (s32[2,1,1,16]{3,2,1,0:T(1,128)S(1)}, s32[2,1,1,16]{3,2,1,0:T(1,128)}, u32[]{:S(2)}) copy-start(s32[2,1,1,16]{3,2,1,0:T(1,128)} %param.8) | copy-start | bytes 388
  0.7 24.3 %copy-start.1 = (bf16[1,1,16,128,128]{4,3,2,1,0:T(8,128)(2,1)S(1)}, bf16[1,1,16,128,128]{4,3,2,1,0:T(8,128)(2,1)}, u32[]{:S(2)}) copy-start(bf16[1,1,16,128,128]{4,3,2,1,0:T(8,128)(2,1)} %param.7) | copy-start | bytes 1572868
  1.8 12.7 %collective-permute-start.2 = (bf16[2,128,128]{2,1,0:T(8,128)(2,1)S(1)}, bf16[2,128,128]{2,1,0:T(8,128)(2,1)S(1)}, u32[]{:S(2)}, u32[]{:S(2)}) collective-permute-start(bf16[2,128,128]{2,1,0:T(8,128)(2,1)S(1)} %slice.33), channel_id=1, source_target_pairs={{33,0},{34,1},{35,2},{36,3},{37,4},{38,5},{39,6},{40,7},{41,8},{42... | collective-permute-start | bytes 196616 | tf_op jit(solution)/shard_map/ppermute | solution.py:22
  3.2 14.7 %collective-permute-start = (bf16[2,256,128]{2,1,0:T(8,128)(2,1)S(1)}, bf16[2,256,128]{2,1,0:T(8,128)(2,1)S(1)}, u32[]{:S(2)}, u32[]{:S(2)}) collective-permute-start(bf16[2,256,128]{2,1,0:T(8,128)(2,1)S(1)} %slice.31), channel_id=1, source_target_pairs={{1,0},{2,1},{3,2},{4,3},{5,4},{6,5},{7,6},{8,7},{9,8},{10,9},{11,1... | collective-permute-start | bytes 393224 | tf_op jit(solution)/shard_map/ppermute | solution.py:22
  4.5 20.5 %collective-permute-start.1 = (bf16[2,128,256]{2,1,0:T(8,128)(2,1)S(1)}, bf16[2,128,256]{2,1,0:T(8,128)(2,1)S(1)}, u32[]{:S(2)}, u32[]{:S(2)}) collective-permute-start(bf16[2,128,256]{2,1,0:T(8,128)(2,1)S(1)} %slice.32), channel_id=1, source_target_pairs={{32,0},{64,32},{96,64},{128,96},{160,128},{192,160},{224,192},{256... | collective-permute-start | bytes 393224 | tf_op jit(solution)/shard_map/ppermute | solution.py:22
  27.4 17.9 %collective-permute-start.3 = (bf16[2,384,128]{2,1,0:T(8,128)(2,1)S(1)}, bf16[2,384,128]{2,1,0:T(8,128)(2,1)S(1)}, u32[]{:S(2)}, u32[]{:S(2)}) collective-permute-start(bf16[2,384,128]{2,1,0:T(8,128)(2,1)S(1)} %get-tuple-element.23), channel_id=1, source_target_pairs={{0,1},{1,2},{2,3},{3,4},{4,5},{5,6},{6,7},{7,8},{8,9},{9,10},{10,1... | collective-permute-start | bytes 589832 | tf_op jit(solution)/shard_map/ppermute | solution.py:22
  33.4 11.9 %collective-permute-start.4 = (bf16[2,384,128]{2,1,0:T(8,128)(2,1)S(1)}, bf16[2,384,128]{2,1,0:T(8,128)(2,1)S(1)}, u32[]{:S(2)}, u32[]{:S(2)}) collective-permute-start(bf16[2,384,128]{2,1,0:T(8,128)(2,1)S(1)} %get-tuple-element.24), channel_id=1, source_target_pairs={{1,0},{2,1},{3,2},{4,3},{5,4},{6,5},{7,6},{8,7},{9,8},{10,9},{11,1... | collective-permute-start | bytes 589832 | tf_op jit(solution)/shard_map/ppermute | solution.py:22
  35.6 5.9 %collective-permute-start.5 = (bf16[1,384,128]{2,1,0:T(8,128)(2,1)S(1)}, bf16[1,384,128]{2,1,0:T(8,128)(2,1)S(1)}, u32[]{:S(2)}, u32[]{:S(2)}) collective-permute-start(bf16[1,384,128]{2,1,0:T(8,128)(2,1)S(1)} %get-tuple-element.25), channel_id=1, source_target_pairs={{0,1},{1,2},{2,3},{3,4},{4,5},{5,6},{6,7},{7,8},{8,9},{9,10},{10,1... | collective-permute-start | bytes 294920 | tf_op jit(solution)/shard_map/ppermute | solution.py:22
  39.9 5.4 %collective-permute-start.6 = (bf16[1,384,128]{2,1,0:T(8,128)(2,1)S(1)}, bf16[1,384,128]{2,1,0:T(8,128)(2,1)S(1)}, u32[]{:S(2)}, u32[]{:S(2)}) collective-permute-start(bf16[1,384,128]{2,1,0:T(8,128)(2,1)S(1)} %get-tuple-element.26), channel_id=1, source_target_pairs={{1,0},{2,1},{3,2},{4,3},{5,4},{6,5},{7,6},{8,7},{9,8},{10,9},{11,1... | collective-permute-start | bytes 294920 | tf_op jit(solution)/shard_map/ppermute | solution.py:22
  45.4 6.4 %collective-permute-start.7 = (bf16[3,3,128,128]{3,2,1,0:T(8,128)(2,1)S(1)}, bf16[3,3,128,128]{3,2,1,0:T(8,128)(2,1)S(1)}, u32[]{:S(2)}, u32[]{:S(2)}) collective-permute-start(bf16[3,3,128,128]{3,2,1,0:T(8,128)(2,1)S(1)} %get-tuple-element.27), channel_id=1, source_target_pairs={{0,32},{32,64},{64,96},{96,128},{128,160},{160,192},{192,224},{224... | collective-permute-start | bytes 884744 | tf_op jit(solution)/shard_map/ppermute | solution.py:22
  48.2 8.0 %collective-permute-start.8 = (bf16[3,3,128,128]{3,2,1,0:T(8,128)(2,1)S(1)}, bf16[3,3,128,128]{3,2,1,0:T(8,128)(2,1)S(1)}, u32[]{:S(2)}, u32[]{:S(2)}) collective-permute-start(bf16[3,3,128,128]{3,2,1,0:T(8,128)(2,1)S(1)} %get-tuple-element.28), channel_id=1, source_target_pairs={{32,0},{64,32},{96,64},{128,96},{160,128},{192,160},{224,192},{256... | collective-permute-start | bytes 884744 | tf_op jit(solution)/shard_map/ppermute | solution.py:22
  72.5 20.7 %collective-permute-start.9 = (bf16[2,384,128]{2,1,0:T(8,128)(2,1)S(1)}, bf16[2,384,128]{2,1,0:T(8,128)(2,1)S(1)}, u32[]{:S(2)}, u32[]{:S(2)}) collective-permute-start(bf16[2,384,128]{2,1,0:T(8,128)(2,1)S(1)} %get-tuple-element.35), channel_id=1, source_target_pairs={{0,1},{1,2},{2,3},{3,4},{4,5},{5,6},{6,7},{7,8},{8,9},{9,10},{10,1... | collective-permute-start | bytes 589832 | tf_op jit(solution)/shard_map/ppermute | solution.py:22
  77.0 27.6 %all-to-all-start.1 = ((bf16[32,16,128]{2,1,0:T(8,128)(2,1)}), bf16[32,16,128]{2,1,0:T(8,128)(2,1)S(1)}, u32[]{:S(2)}, u32[]{:S(2)}) async-start(bf16[32,16,128]{2,1,0:T(8,128)(2,1)} %broadcast_in_dim.4), calls=%async_computation.1 | async-start | bytes 262144 | tf_op jit(solution)/shard_map/all_to_all | solution.py:279
  93.2 5.0 %collective-permute-start.10 = (bf16[2,2,128,128]{3,2,1,0:T(8,128)(2,1)S(1)}, bf16[2,2,128,128]{3,2,1,0:T(8,128)(2,1)S(1)}, u32[]{:S(2)}, u32[]{:S(2)}) collective-permute-start(bf16[2,2,128,128]{3,2,1,0:T(8,128)(2,1)S(1)} %pad_maximum_fusion.5), channel_id=1, source_target_pairs={{0,32},{32,64},{64,96},{96,128},{128,160},{160,192},{192,224},{224... | collective-permute-start | bytes 393224 | tf_op jit(solution)/shard_map/ppermute | solution.py:22

commit v2 on v0

--- a/solution.py
+++ b/solution.py
@@ -260,9 +260,7 @@
 
     right = shift(object_field[:, :, :window].astype(HALO), "col", -1)
     low = shift(object_field[:, :window, :].astype(HALO), "row", -1)
-    diagonal = shift(
-        object_field[:, :window, :window].astype(HALO), ("row", "col"), -(across + 1)
-    )
+    diagonal = shift(object_field[:, :window, :window].astype(HALO), ("row", "col"), -(across + 1))
     scratch = [
         pltpu.VMEM((window, window), F32),
         pltpu.VMEM((GROUP, 2, window, window), F32),
@@ -281,13 +279,13 @@
         10**9,
     )(live, spots, object_field, right, low, diagonal, probe, amp, tables)
 
+    from_right = shift(to_left, "col", -1)
     from_left = shift(to_right, "col", 1)
-    from_right = shift(to_left, "col", -1)
     down, up = call(
         middle_kernel, [((3, 3, window, window), TERMS), ((3, 3, window, window), TERMS)], [VM] * 3
     )(dep, from_left, from_right)
+    from_below = shift(up, "row", -1)
     from_above = shift(down, "row", 1)
-    from_below = shift(up, "row", -1)
 
     updated, inverse, dep, to_right, gradient = call(
         second_kernel,
@@ -306,20 +304,20 @@
     rows, cols = lax.axis_size("row"), lax.axis_size("col")
     parts = exchange(gradient.astype(GRAD).reshape(rows, -1, window), "row")
     part = jnp.sum(parts.astype(F32), 0).astype(GRAD)
-    to_right, dep, ignored = lax.optimization_barrier((to_right, dep, part))
+    to_right, dep, _ = lax.optimization_barrier((to_right, dep, part))
     parts = exchange(jnp.broadcast_to(part[None], (cols,) + part.shape), "col")
     from_left = shift(to_right, "col", 1)
     spill = dep[:, :2, tile:, :]
     spill = jnp.concatenate(
         [(spill[:, :1] + from_left[:, None, tile:].astype(F32)), spill[:, 1:]], 1
     ).astype(TERMS)
-    part = jnp.sum(parts.astype(F32), 0)
-    spill, ignored = lax.optimization_barrier((spill, part))
-    parts = exchange(jnp.broadcast_to(part[None], (rows,) + part.shape), "row")
     from_above = shift(spill, "row", 1)
     refined = call(
         finish_kernel, [((2, tile, tile), F32)], [VM] * 5
     )(updated, inverse, dep, from_left, from_above)[0]
+    parts, refined = lax.optimization_barrier((parts, refined))
+    part = jnp.sum(parts.astype(F32), 0)
+    parts = exchange(jnp.broadcast_to(part[None], (rows,) + part.shape), "row")
     new_probe = call(probe_kernel, [(probe.shape, F32)], [VM] * 2)(
         probe, parts.reshape(gradient.shape)
     )[0]

time: 117 us -> 114 us (0.974)
  the two profiles are of different devices: /device:TPU:8 before, /device:TPU:1 now
where the time goes in v2:
time: 114 us; the launch traced here: 113 us
  starting transfers between devices  46.2 us (41%)
  waiting for transfers between devices  30.2 us (26%)
  blocking collectives  25.2 us (22%)
  Pallas kernels  7.34 us (6%)
  other arithmetic  1.86 us (2%)
  between operations  1.53 us (1%)
    ppermute x9, starting transfers between devices, shift(): lax.ppermute(value, axis, [(source, source + steps) for source in range(f...  31.2 us
    all_to_all x2, blocking collectives, exchange(): return lax.all_to_all(parts, axis, 0, 0, tiled=True)  25.2 us
    ppermute x9, waiting for transfers between devices, shift(): lax.ppermute(value, axis, [(source, source + steps) for source in range(f...  24.6 us
    all_to_all x1, starting transfers between devices, exchange(): return lax.all_to_all(parts, axis, 0, 0, tiled=True)  15.1 us
    all_to_all x1, waiting for transfers between devices, exchange(): return lax.all_to_all(parts, axis, 0, 0, tiled=True)  5.54 us
    pallas_call x1, Pallas kernels, sweeps(): call(second_kernel, [((2, 3, wide, window), F32), ((2, tile, window), F32...  2.86 us
    pallas_call x1, Pallas kernels, sweeps(): call(first_kernel, [((2, 3, wide, window), F32), ((3, 3, wide, window), F...  2.67 us
  transfers between devices with their start and end apart: 10, of which 8 were waited for; matrix products, arithmetic and copies ran while one was open for 1% of the time, Pallas kernels for 1%

profile of v2, /device:TPU:1, one launch (start us, length us, event | category | flops | bytes accessed | tf_op | source)
XLA Modules:
  0.0 113.1 jit_solution(631147302191536789)
XLA Ops:
  0.7 1.2 %convert.46 = bf16[2,256,256]{2,1,0:T(8,128)(2,1)S(1)} convert(f32[2,256,256]{2,1,0:T(8,128)} %obj_ref.1) | non-fusion elementwise | flops 131072 | bytes 786432 | tf_op jit(solution)/shard_map/convert.23
  1.8 1.3 %collective-permute-start.2 = (bf16[2,128,128]{2,1,0:T(8,128)(2,1)S(1)}, bf16[2,128,128]{2,1,0:T(8,128)(2,1)S(1)}, u32[]{:S(2)}, u32[]{:S(2)}) collective-permute-start(bf16[2,128,128]{2,1,0:T(8,128)(2,1)S(1)} %slice.33), channel_id=1, source_target_pairs={{33,0},{34,1},{35,2},{36,3},{37,4},{38,5},{39,6},{40,7},{41,8},{42... | collective-permute-start | bytes 196616 | tf_op jit(solution)/shard_map/ppermute | solution.py:22
  3.2 1.3 %collective-permute-start = (bf16[2,256,128]{2,1,0:T(8,128)(2,1)S(1)}, bf16[2,256,128]{2,1,0:T(8,128)(2,1)S(1)}, u32[]{:S(2)}, u32[]{:S(2)}) collective-permute-start(bf16[2,256,128]{2,1,0:T(8,128)(2,1)S(1)} %slice.31), channel_id=1, source_target_pairs={{1,0},{2,1},{3,2},{4,3},{5,4},{6,5},{7,6},{8,7},{9,8},{10,9},{11,1... | collective-permute-start | bytes 393224 | tf_op jit(solution)/shard_map/ppermute | solution.py:22
  4.5 8.7 %collective-permute-start.1 = (bf16[2,128,256]{2,1,0:T(8,128)(2,1)S(1)}, bf16[2,128,256]{2,1,0:T(8,128)(2,1)S(1)}, u32[]{:S(2)}, u32[]{:S(2)}) collective-permute-start(bf16[2,128,256]{2,1,0:T(8,128)(2,1)S(1)} %slice.32), channel_id=1, source_target_pairs={{32,0},{64,32},{96,64},{128,96},{160,128},{192,160},{224,192},{256... | collective-permute-start | bytes 393224 | tf_op jit(solution)/shard_map/ppermute | solution.py:22
  14.5 3.3 %collective-permute-done.right_ref = bf16[2,256,128]{2,1,0:T(8,128)(2,1)S(1)} collective-permute-done((bf16[2,256,128]{2,1,0:T(8,128)(2,1)S(1)}, bf16[2,256,128]{2,1,0:T(8,128)(2,1)S(1)}, u32[]{:S(2)}, u32[]{:S(2)}) %collective-permute-start) | collective-permute-done | bytes 131104 | tf_op jit(solution)/shard_map/ppermute | solution.py:22
  17.8 7.1 %collective-permute-done.1.low_ref = bf16[2,128,256]{2,1,0:T(8,128)(2,1)S(1)} collective-permute-done((bf16[2,128,256]{2,1,0:T(8,128)(2,1)S(1)}, bf16[2,128,256]{2,1,0:T(8,128)(2,1)S(1)}, u32[]{:S(2)}, u32[]{:S(2)}) %collective-permute-start.1) | collective-permute-done | bytes 131104 | tf_op jit(solution)/shard_map/ppermute | solution.py:22
  25.0 2.7 %shard_map.68 = (f32[2,3,384,128]{3,2,1,0:T(8,128)S(1)}, f32[3,3,384,128]{3,2,1,0:T(8,128)S(1)}, bf16[3,384,128]{2,1,0:T(8,128)(2,1)S(1)}, bf16[3,384,128]{2,1,0:T(8,128)(2,1)S(1)}) custom-call(s32[1,1]{1,0:T(1,128)S(6)} %copy.7.live_ref, s32[2,16]{1,0:T(2,128)S(1)} %bitcast.16, f32[2,256,256]{2,1,0:T(8,128)S(1)} %copy-done.2, ...), custom_call_target="tpu_custom_call" | custom-call | flops 1000000000 | bytes 1000000 | tf_op jit(solution)/shard_map/pallas_call | solution.py:269
  27.6 6.4 %collective-permute-start.3 = (bf16[3,384,128]{2,1,0:T(8,128)(2,1)S(1)}, bf16[3,384,128]{2,1,0:T(8,128)(2,1)S(1)}, u32[]{:S(2)}, u32[]{:S(2)}) collective-permute-start(bf16[3,384,128]{2,1,0:T(8,128)(2,1)S(1)} %get-tuple-element.19), channel_id=1, source_target_pairs={{0,1},{1,2},{2,3},{3,4},{4,5},{5,6},{6,7},{7,8},{8,9},{9,10},{10,1... | collective-permute-start | bytes 884744 | tf_op jit(solution)/shard_map/ppermute | solution.py:22
  34.1 1.3 %collective-permute-start.4 = (bf16[3,384,128]{2,1,0:T(8,128)(2,1)S(1)}, bf16[3,384,128]{2,1,0:T(8,128)(2,1)S(1)}, u32[]{:S(2)}, u32[]{:S(2)}) collective-permute-start(bf16[3,384,128]{2,1,0:T(8,128)(2,1)S(1)} %get-tuple-element.20), channel_id=1, source_target_pairs={{1,0},{2,1},{3,2},{4,3},{5,4},{6,5},{7,6},{8,7},{9,8},{10,9},{11,1... | collective-permute-start | bytes 884744 | tf_op jit(solution)/shard_map/ppermute | solution.py:22
  35.4 2.3 %collective-permute-done.3.from_left_ref.left_ref = bf16[3,384,128]{2,1,0:T(8,128)(2,1)S(1)} collective-permute-done((bf16[3,384,128]{2,1,0:T(8,128)(2,1)S(1)}, bf16[3,384,128]{2,1,0:T(8,128)(2,1)S(1)}, u32[]{:S(2)}, u32[]{:S(2)}) %collective-permute-start.3) | collective-permute-done | bytes 294944 | tf_op jit(solution)/shard_map/ppermute | solution.py:22
  37.7 3.8 %collective-permute-done.4.from_right_ref.right_ref = bf16[3,384,128]{2,1,0:T(8,128)(2,1)S(1)} collective-permute-done((bf16[3,384,128]{2,1,0:T(8,128)(2,1)S(1)}, bf16[3,384,128]{2,1,0:T(8,128)(2,1)S(1)}, u32[]{:S(2)}, u32[]{:S(2)}) %collective-permute-start.4) | collective-permute-done | bytes 294944 | tf_op jit(solution)/shard_map/ppermute | solution.py:22
  41.7 3.7 %collective-permute-start.5 = (bf16[3,3,128,128]{3,2,1,0:T(8,128)(2,1)S(1)}, bf16[3,3,128,128]{3,2,1,0:T(8,128)(2,1)S(1)}, u32[]{:S(2)}, u32[]{:S(2)}) collective-permute-start(bf16[3,3,128,128]{3,2,1,0:T(8,128)(2,1)S(1)} %get-tuple-element.21), channel_id=1, source_target_pairs={{0,32},{32,64},{64,96},{96,128},{128,160},{160,192},{192,224},{224... | collective-permute-start | bytes 884744 | tf_op jit(solution)/shard_map/ppermute | solution.py:22
  45.3 1.9 %collective-permute-start.6 = (bf16[3,3,128,128]{3,2,1,0:T(8,128)(2,1)S(1)}, bf16[3,3,128,128]{3,2,1,0:T(8,128)(2,1)S(1)}, u32[]{:S(2)}, u32[]{:S(2)}) collective-permute-start(bf16[3,3,128,128]{3,2,1,0:T(8,128)(2,1)S(1)} %get-tuple-element.22), channel_id=1, source_target_pairs={{32,0},{64,32},{96,64},{128,96},{160,128},{192,160},{224,192},{256... | collective-permute-start | bytes 884744 | tf_op jit(solution)/shard_map/ppermute | solution.py:22
  47.3 1.7 %collective-permute-done.5.above_ref = bf16[3,3,128,128]{3,2,1,0:T(8,128)(2,1)S(1)} collective-permute-done((bf16[3,3,128,128]{3,2,1,0:T(8,128)(2,1)S(1)}, bf16[3,3,128,128]{3,2,1,0:T(8,128)(2,1)S(1)}, u32[]{:S(2)}, u32[]{:S(2)}) %collective-permute-start.5) | collective-permute-done | bytes 294944 | tf_op jit(solution)/shard_map/ppermute | solution.py:22
  49.0 4.4 %collective-permute-done.6.below_ref = bf16[3,3,128,128]{3,2,1,0:T(8,128)(2,1)S(1)} collective-permute-done((bf16[3,3,128,128]{3,2,1,0:T(8,128)(2,1)S(1)}, bf16[3,3,128,128]{3,2,1,0:T(8,128)(2,1)S(1)}, u32[]{:S(2)}, u32[]{:S(2)}) %collective-permute-start.6) | collective-permute-done | bytes 294944 | tf_op jit(solution)/shard_map/ppermute | solution.py:22
  53.4 2.9 %shard_map.70 = (f32[2,3,384,128]{3,2,1,0:T(8,128)S(1)}, f32[2,256,128]{2,1,0:T(8,128)S(1)}, f32[2,3,384,128]{3,2,1,0:T(8,128)S(1)}, bf16[2,384,128]{2,1,0:T(8,128)(2,1)S(1)}, f32[2,128,128]{2,1,0:T(8,128)S(1)}) custom-call(s32[1,1]{1,0:T(1,128)S(6)} %copy.7.live_ref, s32[2,16]{1,0:T(2,128)S(1)} %bitcast.17, ...), custom_call_target="tpu_custom_call" | custom-call | flops 1000000000 | bytes 1000000 | tf_op jit(solution)/shard_map/pallas_call | solution.py:290
  56.3 14.4 %all_to_all.15 = bf16[16,16,128]{2,1,0:T(8,128)(2,1)S(1)} all-to-all(bf16[16,16,128]{2,1,0:T(8,128)(2,1)S(1)} %bitcast.18), channel_id=1, replica_groups=mesh['row'=16,'col'=32] {'row'}, dimensions={0} | all-to-all | bytes 131072 | tf_op jit(solution)/shard_map/all_to_all | solution.py:247
  70.7 3.5 %collective-permute-start.7 = (bf16[2,384,128]{2,1,0:T(8,128)(2,1)S(1)}, bf16[2,384,128]{2,1,0:T(8,128)(2,1)S(1)}, u32[]{:S(2)}, u32[]{:S(2)}) collective-permute-start(bf16[2,384,128]{2,1,0:T(8,128)(2,1)S(1)} %get-tuple-element.29), channel_id=1, source_target_pairs={{0,1},{1,2},{2,3},{3,4},{4,5},{5,6},{6,7},{7,8},{8,9},{9,10},{10,1... | collective-permute-start | bytes 589832 | tf_op jit(solution)/shard_map/ppermute | solution.py:22
  74.9 15.1 %all-to-all-start.1 = ((bf16[32,16,128]{2,1,0:T(8,128)(2,1)}), bf16[32,16,128]{2,1,0:T(8,128)(2,1)S(1)}, u32[]{:S(2)}, u32[]{:S(2)}) async-start(bf16[32,16,128]{2,1,0:T(8,128)(2,1)} %broadcast_in_dim.4), calls=%async_computation.1 | async-start | bytes 262144 | tf_op jit(solution)/shard_map/all_to_all | solution.py:247
  90.0 3.0 %collective-permute-start.8 = (bf16[2,2,128,128]{3,2,1,0:T(8,128)(2,1)S(1)}, bf16[2,2,128,128]{3,2,1,0:T(8,128)(2,1)S(1)}, u32[]{:S(2)}, u32[]{:S(2)}) collective-permute-start(bf16[2,2,128,128]{3,2,1,0:T(8,128)(2,1)S(1)} %pad_maximum_fusion.5), channel_id=1, source_target_pairs={{0,32},{32,64},{64,96},{96,128},{128,160},{160,192},{192,224},{224... | collective-permute-start | bytes 393224 | tf_op jit(solution)/shard_map/ppermute | solution.py:22
  93.1 1.9 %collective-permute-done.8.above_ref = bf16[2,2,128,128]{3,2,1,0:T(8,128)(2,1)S(1)} collective-permute-done((bf16[2,2,128,128]{3,2,1,0:T(8,128)(2,1)S(1)}, bf16[2,2,128,128]{3,2,1,0:T(8,128)(2,1)S(1)}, u32[]{:S(2)}, u32[]{:S(2)}) %collective-permute-start.8) | collective-permute-done | bytes 131104 | tf_op jit(solution)/shard_map/ppermute | solution.py:22
  95.0 0.9 shard_map.71
  95.9 5.5 %all-to-all-done.1 = bf16[32,16,128]{2,1,0:T(8,128)(2,1)S(1)} async-done(((bf16[32,16,128]{2,1,0:T(8,128)(2,1)}), bf16[32,16,128]{2,1,0:T(8,128)(2,1)S(1)}, u32[]{:S(2)}, u32[]{:S(2)}) %all-to-all-start.1) | async-done | bytes 131104 | tf_op jit(solution)/shard_map/all_to_all | solution.py:247
  101.5 10.8 %all_to_all.16 = f32[16,16,128]{2,1,0:T(8,128)S(1)} all-to-all(f32[16,16,128]{2,1,0:T(8,128)S(1)} %broadcast_in_dim.5), channel_id=1, replica_groups=mesh['row'=16,'col'=32] {'row'}, dimensions={0} | all-to-all | bytes 262144 | tf_op jit(solution)/shard_map/all_to_all | solution.py:247
  (27 shorter events, 2.4 us)
Async XLA Ops:
  0.6 24.3 %copy-start.2 = (f32[2,256,256]{2,1,0:T(8,128)S(1)}, f32[2,256,256]{2,1,0:T(8,128)}, u32[]{:S(2)}) copy-start(f32[2,256,256]{2,1,0:T(8,128)} %obj_ref.1) | copy-start | bytes 1572868
  0.6 24.3 %copy-start.1 = (f32[2,128,128]{2,1,0:T(8,128)S(1)}, f32[2,128,128]{2,1,0:T(8,128)}, u32[]{:S(2)}) copy-start(f32[2,128,128]{2,1,0:T(8,128)} %probe_ref.5) | copy-start | bytes 393220
  0.7 24.3 %copy-start.3 = (s32[2,1,1,16]{3,2,1,0:T(1,128)S(1)}, s32[2,1,1,16]{3,2,1,0:T(1,128)}, u32[]{:S(2)}) copy-start(s32[2,1,1,16]{3,2,1,0:T(1,128)} %param.8) | copy-start | bytes 388
  0.7 24.3 %copy-start = (bf16[1,1,16,128,128]{4,3,2,1,0:T(8,128)(2,1)S(1)}, bf16[1,1,16,128,128]{4,3,2,1,0:T(8,128)(2,1)}, u32[]{:S(2)}) copy-start(bf16[1,1,16,128,128]{4,3,2,1,0:T(8,128)(2,1)} %param.7) | copy-start | bytes 1572868
  1.8 12.7 %collective-permute-start.2 = (bf16[2,128,128]{2,1,0:T(8,128)(2,1)S(1)}, bf16[2,128,128]{2,1,0:T(8,128)(2,1)S(1)}, u32[]{:S(2)}, u32[]{:S(2)}) collective-permute-start(bf16[2,128,128]{2,1,0:T(8,128)(2,1)S(1)} %slice.33), channel_id=1, source_target_pairs={{33,0},{34,1},{35,2},{36,3},{37,4},{38,5},{39,6},{40,7},{41,8},{42... | collective-permute-start | bytes 196616 | tf_op jit(solution)/shard_map/ppermute | solution.py:22
  3.2 14.7 %collective-permute-start = (bf16[2,256,128]{2,1,0:T(8,128)(2,1)S(1)}, bf16[2,256,128]{2,1,0:T(8,128)(2,1)S(1)}, u32[]{:S(2)}, u32[]{:S(2)}) collective-permute-start(bf16[2,256,128]{2,1,0:T(8,128)(2,1)S(1)} %slice.31), channel_id=1, source_target_pairs={{1,0},{2,1},{3,2},{4,3},{5,4},{6,5},{7,6},{8,7},{9,8},{10,9},{11,1... | collective-permute-start | bytes 393224 | tf_op jit(solution)/shard_map/ppermute | solution.py:22
  4.5 20.5 %collective-permute-start.1 = (bf16[2,128,256]{2,1,0:T(8,128)(2,1)S(1)}, bf16[2,128,256]{2,1,0:T(8,128)(2,1)S(1)}, u32[]{:S(2)}, u32[]{:S(2)}) collective-permute-start(bf16[2,128,256]{2,1,0:T(8,128)(2,1)S(1)} %slice.32), channel_id=1, source_target_pairs={{32,0},{64,32},{96,64},{128,96},{160,128},{192,160},{224,192},{256... | collective-permute-start | bytes 393224 | tf_op jit(solution)/shard_map/ppermute | solution.py:22
  27.6 10.1 %collective-permute-start.3 = (bf16[3,384,128]{2,1,0:T(8,128)(2,1)S(1)}, bf16[3,384,128]{2,1,0:T(8,128)(2,1)S(1)}, u32[]{:S(2)}, u32[]{:S(2)}) collective-permute-start(bf16[3,384,128]{2,1,0:T(8,128)(2,1)S(1)} %get-tuple-element.19), channel_id=1, source_target_pairs={{0,1},{1,2},{2,3},{3,4},{4,5},{5,6},{6,7},{7,8},{8,9},{9,10},{10,1... | collective-permute-start | bytes 884744 | tf_op jit(solution)/shard_map/ppermute | solution.py:22
  34.1 7.5 %collective-permute-start.4 = (bf16[3,384,128]{2,1,0:T(8,128)(2,1)S(1)}, bf16[3,384,128]{2,1,0:T(8,128)(2,1)S(1)}, u32[]{:S(2)}, u32[]{:S(2)}) collective-permute-start(bf16[3,384,128]{2,1,0:T(8,128)(2,1)S(1)} %get-tuple-element.20), channel_id=1, source_target_pairs={{1,0},{2,1},{3,2},{4,3},{5,4},{6,5},{7,6},{8,7},{9,8},{10,9},{11,1... | collective-permute-start | bytes 884744 | tf_op jit(solution)/shard_map/ppermute | solution.py:22
  41.7 7.3 %collective-permute-start.5 = (bf16[3,3,128,128]{3,2,1,0:T(8,128)(2,1)S(1)}, bf16[3,3,128,128]{3,2,1,0:T(8,128)(2,1)S(1)}, u32[]{:S(2)}, u32[]{:S(2)}) collective-permute-start(bf16[3,3,128,128]{3,2,1,0:T(8,128)(2,1)S(1)} %get-tuple-element.21), channel_id=1, source_target_pairs={{0,32},{32,64},{64,96},{96,128},{128,160},{160,192},{192,224},{224... | collective-permute-start | bytes 884744 | tf_op jit(solution)/shard_map/ppermute | solution.py:22
  45.3 8.0 %collective-permute-start.6 = (bf16[3,3,128,128]{3,2,1,0:T(8,128)(2,1)S(1)}, bf16[3,3,128,128]{3,2,1,0:T(8,128)(2,1)S(1)}, u32[]{:S(2)}, u32[]{:S(2)}) collective-permute-start(bf16[3,3,128,128]{3,2,1,0:T(8,128)(2,1)S(1)} %get-tuple-element.22), channel_id=1, source_target_pairs={{32,0},{64,32},{96,64},{128,96},{160,128},{192,160},{224,192},{256... | collective-permute-start | bytes 884744 | tf_op jit(solution)/shard_map/ppermute | solution.py:22
  70.7 19.3 %collective-permute-start.7 = (bf16[2,384,128]{2,1,0:T(8,128)(2,1)S(1)}, bf16[2,384,128]{2,1,0:T(8,128)(2,1)S(1)}, u32[]{:S(2)}, u32[]{:S(2)}) collective-permute-start(bf16[2,384,128]{2,1,0:T(8,128)(2,1)S(1)} %get-tuple-element.29), channel_id=1, source_target_pairs={{0,1},{1,2},{2,3},{3,4},{4,5},{5,6},{6,7},{7,8},{8,9},{9,10},{10,1... | collective-permute-start | bytes 589832 | tf_op jit(solution)/shard_map/ppermute | solution.py:22
  74.9 26.5 %all-to-all-start.1 = ((bf16[32,16,128]{2,1,0:T(8,128)(2,1)}), bf16[32,16,128]{2,1,0:T(8,128)(2,1)S(1)}, u32[]{:S(2)}, u32[]{:S(2)}) async-start(bf16[32,16,128]{2,1,0:T(8,128)(2,1)} %broadcast_in_dim.4), calls=%async_computation.1 | async-start | bytes 262144 | tf_op jit(solution)/shard_map/all_to_all | solution.py:247
  90.0 5.0 %collective-permute-start.8 = (bf16[2,2,128,128]{3,2,1,0:T(8,128)(2,1)S(1)}, bf16[2,2,128,128]{3,2,1,0:T(8,128)(2,1)S(1)}, u32[]{:S(2)}, u32[]{:S(2)}) collective-permute-start(bf16[2,2,128,128]{3,2,1,0:T(8,128)(2,1)S(1)} %pad_maximum_fusion.5), channel_id=1, source_target_pairs={{0,32},{32,64},{64,96},{96,128},{128,160},{160,192},{192,224},{224... | collective-permute-start | bytes 393224 | tf_op jit(solution)/shard_map/ppermute | solution.py:22
